TPU v7x, 32 devices: a whole 2x2x4 slice. The times are simulated.
32 devices in a mesh: dp: 4 (over y, core), ctx: 4 (over z), tp: 2 (over x).
Axes of the slice: x: 2, y: 2, z: 4, core: 2. Of those that a mesh axis runs over, the one named last changes fastest.
Arguments:
- img_in: bfloat16 [4, 512, 1536], P('dp', 'ctx'), may hold values from -6 to 6
- txt_in: bfloat16 [4, 154, 1536], P('dp'), may hold values from -6 to 6
- cond: bfloat16 [4, 1536], P(None, ('dp', 'ctx', 'tp')), may hold values from -6 to 6
- mod_weight: float32 [1, 2, 1536, 6, 1536], P(None, None, ('dp', 'ctx', 'tp')), may hold values from -0.15625 to 0.15625
- qkv_weight: float32 [1, 2, 1536, 3, 1536], P(None, None, ('dp', 'ctx'), None, 'tp'), may hold values from -0.15625 to 0.15625
- out_weight: float32 [1, 2, 1536, 1536], P(None, None, 'tp', ('dp', 'ctx')), may hold values from -0.75 to 0.75
- up_weight: float32 [1, 2, 1536, 6144], P(None, None, ('dp', 'ctx'), 'tp'), may hold values from -0.15625 to 0.15625
- down_weight: float32 [1, 2, 6144, 1536], P(None, None, 'tp', ('dp', 'ctx')), may hold values from -0.078125 to 0.078125
- norm_gain: float32 [1, 2, 2, 64], replicated, may hold values from 0.7 to 1.8
- cot_img: bfloat16 [4, 512, 1536], P('dp', 'ctx'), may hold values from -6 to 6
- cot_txt: bfloat16 [4, 154, 1536], P('dp'), may hold values from -6 to 6
- mod_moment: float32 [1, 2, 1536, 6, 1536], P(None, None, ('dp', 'ctx', 'tp')), may hold values from -6 to 6
- qkv_moment: float32 [1, 2, 1536, 3, 1536], P(None, None, ('dp', 'ctx'), None, 'tp'), may hold values from -6 to 6
- out_moment: float32 [1, 2, 1536, 1536], P(None, None, 'tp', ('dp', 'ctx')), may hold values from -6 to 6
- up_moment: float32 [1, 2, 1536, 6144], P(None, None, ('dp', 'ctx'), 'tp'), may hold values from -6 to 6
- down_moment: float32 [1, 2, 6144, 1536], P(None, None, 'tp', ('dp', 'ctx')), may hold values from -6 to 6
- gain_moment: float32 [1, 2, 2, 64], replicated, may hold values from -6 to 6
- mod_second: float32 [1, 2, 1536, 6, 1536], P(None, None, ('dp', 'ctx', 'tp')), may hold values from 0.5 to 2
- qkv_second: float32 [1, 2, 1536, 3, 1536], P(None, None, ('dp', 'ctx'), None, 'tp'), may hold values from 0.5 to 2
- out_second: float32 [1, 2, 1536, 1536], P(None, None, 'tp', ('dp', 'ctx')), may hold values from 0.5 to 2
- up_second: float32 [1, 2, 1536, 6144], P(None, None, ('dp', 'ctx'), 'tp'), may hold values from 0.5 to 2
- down_second: float32 [1, 2, 6144, 1536], P(None, None, 'tp', ('dp', 'ctx')), may hold values from 0.5 to 2
- gain_second: float32 [1, 2, 2, 64], replicated, may hold values from 0.5 to 2
Outputs:
- img_out: bfloat16 [4, 512, 1536], P('dp', 'ctx')
- txt_out: bfloat16 [4, 154, 1536], P('dp')
- img_grad: bfloat16 [4, 512, 1536], P('dp', 'ctx')
- txt_grad: bfloat16 [4, 154, 1536], P('dp')
- mod_grad: float32 [1, 2, 1536, 6, 1536], P(None, None, ('dp', 'ctx', 'tp'))
- mod_next: float32 [1, 2, 1536, 6, 1536], P(None, None, ('dp', 'ctx', 'tp'))
- mod_moment_next: float32 [1, 2, 1536, 6, 1536], P(None, None, ('dp', 'ctx', 'tp'))
- mod_second_next: float32 [1, 2, 1536, 6, 1536], P(None, None, ('dp', 'ctx', 'tp'))
- qkv_grad: float32 [1, 2, 1536, 3, 1536], P(None, None, ('dp', 'ctx'), None, 'tp')
- qkv_next: float32 [1, 2, 1536, 3, 1536], P(None, None, ('dp', 'ctx'), None, 'tp')
- qkv_moment_next: float32 [1, 2, 1536, 3, 1536], P(None, None, ('dp', 'ctx'), None, 'tp')
- qkv_second_next: float32 [1, 2, 1536, 3, 1536], P(None, None, ('dp', 'ctx'), None, 'tp')
- out_grad: float32 [1, 2, 1536, 1536], P(None, None, 'tp', ('dp', 'ctx'))
- out_next: float32 [1, 2, 1536, 1536], P(None, None, 'tp', ('dp', 'ctx'))
- out_moment_next: float32 [1, 2, 1536, 1536], P(None, None, 'tp', ('dp', 'ctx'))
- out_second_next: float32 [1, 2, 1536, 1536], P(None, None, 'tp', ('dp', 'ctx'))
- up_grad: float32 [1, 2, 1536, 6144], P(None, None, ('dp', 'ctx'), 'tp')
- up_next: float32 [1, 2, 1536, 6144], P(None, None, ('dp', 'ctx'), 'tp')
- up_moment_next: float32 [1, 2, 1536, 6144], P(None, None, ('dp', 'ctx'), 'tp')
- up_second_next: float32 [1, 2, 1536, 6144], P(None, None, ('dp', 'ctx'), 'tp')
- down_grad: float32 [1, 2, 6144, 1536], P(None, None, 'tp', ('dp', 'ctx'))
- down_next: float32 [1, 2, 6144, 1536], P(None, None, 'tp', ('dp', 'ctx'))
- down_moment_next: float32 [1, 2, 6144, 1536], P(None, None, 'tp', ('dp', 'ctx'))
- down_second_next: float32 [1, 2, 6144, 1536], P(None, None, 'tp', ('dp', 'ctx'))
- gain_grad: float32 [1, 2, 2, 64], replicated
- gain_next: float32 [1, 2, 2, 64], replicated
- gain_moment_next: float32 [1, 2, 2, 64], replicated
- gain_second_next: float32 [1, 2, 2, 64], replicated
All inputs are finite; a program needn't handle non-finite values.
Results may differ from a plain program's by a relative error of at most 0.025.
Values may be sent and summed in bfloat16 or wider, within the bound.
A program may use at most 320 MiB of HBM per device.

v0:
```python
import functools
from types import SimpleNamespace as NS

import jax
import jax.numpy as jnp
from jax import lax
from jax.experimental import pallas as pl
from jax.experimental.pallas import tpu as pltpu
from jax.sharding import PartitionSpec as P

DP, CTX, TP = "dp", "ctx", "tp"
ROWS = (DP, CTX)
ALL = (DP, CTX, TP)

norm_eps = 1e-06
learn_rate = 0.004
beta_one = 0.9
beta_two = 0.999
adam_eps = 1e-08
decay_rate = 0.1
corr_one = 1.0 - beta_one**3
corr_two = 1.0 - beta_two**3

BF = jnp.bfloat16
F32 = jnp.float32


def product(pattern, former, latter):
    return jnp.einsum(pattern, former, latter, preferred_element_type=jnp.float32)


def layer_norm(values):
    center = values - jnp.mean(values, axis=-1, keepdims=True)
    spread = lax.rsqrt(jnp.mean(center * center, axis=-1, keepdims=True) + norm_eps)
    return (center * spread, spread)


def norm_back(incoming, normed, spread):
    return spread * (
        incoming
        - jnp.mean(incoming, axis=-1, keepdims=True)
        - normed * jnp.mean(incoming * normed, axis=-1, keepdims=True)
    )


def rms_norm(raw_rows):
    factor = lax.rsqrt(jnp.mean(raw_rows * raw_rows, axis=-1, keepdims=True) + norm_eps)
    return (raw_rows * factor, factor)


def rms_back(incoming, normed, factor):
    return factor * (incoming - normed * jnp.mean(incoming * normed, axis=-1, keepdims=True))


def gelu_tanh(values):
    return jax.nn.gelu(values, approximate=True)


def adam_step(weight, moment, second, gradient):
    new_moment = beta_one * moment + (1.0 - beta_one) * gradient
    new_second = beta_two * second + (1.0 - beta_two) * gradient * gradient
    update = (
        new_moment / corr_one / (jnp.sqrt(new_second / corr_two) + adam_eps) + decay_rate * weight
    )
    return (weight - learn_rate * update, new_moment, new_second)


def modulate(normed, shift_vec, scale_vec):
    return (normed * (1.0 + scale_vec[:, None, :]) + shift_vec[:, None, :]).astype(jnp.bfloat16)


def stream_front(inputs, modulation, qkv_part, gain_pair):
    values = inputs.astype(jnp.float32)
    normed, spread = layer_norm(values)
    hidden = modulate(normed, modulation[:, 0], modulation[:, 1])
    packed = product("btd,dkc->btkc", hidden, qkv_part)
    packed = packed.reshape(packed.shape[0], packed.shape[1], 3, -1, gain_pair.shape[-1])
    q_hat, q_factor = rms_norm(packed[:, :, 0])
    k_hat, k_factor = rms_norm(packed[:, :, 1])
    return NS(        values=values,
        normed=normed,
        spread=spread,
        hidden=hidden,
        q_hat=q_hat,
        q_factor=q_factor,
        k_hat=k_hat,
        k_factor=k_factor,
        queries=(q_hat * gain_pair[0]).astype(jnp.bfloat16),
        key_rows=(k_hat * gain_pair[1]).astype(jnp.bfloat16),
        value_rows=packed[:, :, 2].astype(jnp.bfloat16),)


def mlp_front(resid, modulation, up_part):
    normed, spread = layer_norm(resid)
    hidden = modulate(normed, modulation[:, 3], modulation[:, 4])
    pre_act = product("btd,df->btf", hidden, up_part)
    activated = gelu_tanh(pre_act).astype(jnp.bfloat16)
    return NS(        normed=normed,
        spread=spread,
        hidden=hidden,
        pre_act=pre_act,
        activated=activated,)


def attend(query_all, key_all, value_all, scale_factor):
    scores = product("bqhd,bkhd->bhqk", query_all, key_all) * scale_factor
    row_peak = jnp.max(scores, axis=-1, keepdims=True)
    log_total = row_peak + jnp.log(jnp.sum(jnp.exp(scores - row_peak), axis=-1, keepdims=True))
    attn_probs = jnp.exp(scores - log_total).astype(jnp.bfloat16)
    attended = product("bhqk,bkhd->bqhd", attn_probs, value_all)
    return (attended, log_total)


def attend_back(
    grad_att, query_all, key_all, value_all, attended, log_total, scale_factor, split_at
):
    row_delta = jnp.sum(grad_att.astype(jnp.float32) * attended, axis=-1)
    scores = product("bqhd,bkhd->bhqk", query_all, key_all) * scale_factor
    attn_probs = jnp.exp(scores - log_total)
    prob_grad = product("bqhd,bkhd->bhqk", grad_att, value_all)
    score_grad = (
        attn_probs * (prob_grad - jnp.transpose(row_delta, (0, 2, 1))[..., None]) * scale_factor
    ).astype(jnp.bfloat16)
    probs_low = attn_probs.astype(jnp.bfloat16)
    query_grad = product("bhqk,bkhd->bqhd", score_grad, key_all)
    key_first = product("bhqk,bqhd->bkhd", score_grad[:, :, :split_at], query_all[:, :split_at])
    key_second = product("bhqk,bqhd->bkhd", score_grad[:, :, split_at:], query_all[:, split_at:])
    value_first = product("bhqk,bqhd->bkhd", probs_low[:, :, :split_at], grad_att[:, :split_at])
    value_second = product("bhqk,bqhd->bkhd", probs_low[:, :, split_at:], grad_att[:, split_at:])
    return (query_grad, key_first, key_second, value_first, value_second)


def mlp_back(grad_out, modulation, mlp_parts, down_out, up_part, down_part):
    gate_two = jnp.sum(grad_out * down_out, axis=1)
    branch = (grad_out * modulation[:, 5][:, None, :]).astype(jnp.bfloat16)
    act_grad = product("btd,fd->btf", branch, down_part)
    down_term = product("btf,btd->fd", mlp_parts.activated, branch)
    pre_grad = jax.vjp(gelu_tanh, mlp_parts.pre_act)[1](act_grad)[0].astype(jnp.bfloat16)
    up_term = product("btd,btf->df", mlp_parts.hidden, pre_grad)
    hidden_part = product("btf,df->btd", pre_grad, up_part)
    return (gate_two, down_term, up_term, hidden_part)


def norm_branch_back(hidden_grad, normed, spread, scale_vec, residual_grad):
    shift_grad = jnp.sum(hidden_grad, axis=1)
    scale_grad = jnp.sum(hidden_grad * normed, axis=1)
    total = residual_grad + norm_back(hidden_grad * (1.0 + scale_vec[:, None, :]), normed, spread)
    return (shift_grad, scale_grad, total)


def attention_branch_back(resid_grad, modulation, proj, flat_rows, out_part):
    gate_one = jnp.sum(resid_grad * proj, axis=1)
    branch = (resid_grad * modulation[:, 2][:, None, :]).astype(jnp.bfloat16)
    att_grad = product("btd,cd->btc", branch, out_part)
    out_term = product("btc,btd->cd", flat_rows, branch)
    return (gate_one, att_grad, out_term)


def head_back(query_grad, key_grad, value_grad, front, gain_pair):
    gain_term = jnp.stack(
        [
            jnp.sum(query_grad * front.q_hat, axis=(0, 1, 2)),
            jnp.sum(key_grad * front.k_hat, axis=(0, 1, 2)),
        ]
    )
    q_raw = rms_back(query_grad * gain_pair[0], front.q_hat, front.q_factor)
    k_raw = rms_back(key_grad * gain_pair[1], front.k_hat, front.k_factor)
    packed = jnp.stack([q_raw, k_raw, value_grad], axis=2)
    packed = packed.reshape(packed.shape[0], packed.shape[1], 3, -1).astype(jnp.bfloat16)
    return (gain_term, packed)


def gathered_body(
    img_in,
    txt_in,
    cond,
    mod_weight,
    qkv_weight,
    out_weight,
    up_weight,
    down_weight,
    norm_gain,
    cot_img,
    cot_txt,
    mod_moment,
    qkv_moment,
    out_moment,
    up_moment,
    down_moment,
    gain_moment,
    mod_second,
    qkv_second,
    out_second,
    up_second,
    down_second,
    gain_second,
):
    ctx_count = lax.axis_size(CTX)
    tp_count = lax.axis_size(TP)
    seq_dev = img_in.shape[0]
    img_dev = img_in.shape[1]
    txt_rows = txt_in.shape[1]
    img_total = img_dev * ctx_count
    layer_count = qkv_weight.shape[0]
    head_dim = norm_gain.shape[-1]
    scale_factor = head_dim ** (-0.5)
    seq_start = lax.axis_index(DP) * seq_dev
    ctx_start = lax.axis_index(CTX) * img_dev
    cond_act = jax.nn.silu(cond.astype(jnp.float32)).astype(jnp.bfloat16)
    mod_part = product("sm,ltmkc->ltskc", cond_act, mod_weight.astype(jnp.bfloat16))
    all_mod = lax.psum(mod_part, ALL)
    own_mod = lax.dynamic_slice_in_dim(all_mod, seq_start, seq_dev, 2)

    def gather_weights(layer_id):
        return (
            lax.all_gather(
                qkv_weight[layer_id].astype(jnp.bfloat16), ROWS, axis=1, tiled=True
            ),
            lax.all_gather(
                out_weight[layer_id].astype(jnp.bfloat16), ROWS, axis=2, tiled=True
            ),
            lax.all_gather(
                up_weight[layer_id].astype(jnp.bfloat16), ROWS, axis=1, tiled=True
            ),
            lax.all_gather(
                down_weight[layer_id].astype(jnp.bfloat16), ROWS, axis=2, tiled=True
            ),
        )

    def joined_keys(front_pair):
        remote_keys, remote_values = (
            lax.all_gather(front_pair[0].key_rows, CTX, axis=1, tiled=True),
            lax.all_gather(front_pair[0].value_rows, CTX, axis=1, tiled=True),
        )
        key_all = jnp.concatenate([remote_keys, front_pair[1].key_rows], axis=1)
        value_all = jnp.concatenate([remote_values, front_pair[1].value_rows], axis=1)
        return (key_all, value_all)

    streams = [img_in, txt_in]
    layer_id = 0
    full_qkv, full_out, full_up, full_down = gather_weights(layer_id)
    mod_pair = [own_mod[layer_id, 0], own_mod[layer_id, 1]]
    front_pair = [
        stream_front(
            streams[stream_id],
            mod_pair[stream_id],
            full_qkv[stream_id],
            norm_gain[layer_id, stream_id],
        )
        for stream_id in range(2)
    ]
    key_all, value_all = joined_keys(front_pair)
    query_all = jnp.concatenate([front_pair[0].queries, front_pair[1].queries], axis=1)
    attended, log_total = attend(query_all, key_all, value_all, scale_factor)
    attended_low = attended.astype(jnp.bfloat16)
    flat_pair = [
        attended_low[:, :img_dev].reshape(seq_dev, img_dev, -1),
        attended_low[:, img_dev:].reshape(seq_dev, txt_rows, -1),
    ]
    proj_img = lax.psum(
        product("btc,cd->btd", flat_pair[0], full_out[0]).astype(jnp.bfloat16), TP
    ).astype(jnp.float32)
    proj_txt = lax.psum(
        product("btc,cd->btd", flat_pair[1], full_out[1]).astype(jnp.bfloat16), TP
    ).astype(jnp.float32)
    proj_pair = [proj_img, proj_txt]
    resid_pair = [
        front_pair[stream_id].values
        + mod_pair[stream_id][:, 2][:, None, :] * proj_pair[stream_id]
        for stream_id in range(2)
    ]
    mlp_pair = [
        mlp_front(resid_pair[stream_id], mod_pair[stream_id], full_up[stream_id])
        for stream_id in range(2)
    ]
    down_img = lax.psum(
        product("btf,fd->btd", mlp_pair[0].activated, full_down[0]).astype(jnp.bfloat16), TP
    ).astype(jnp.float32)
    down_txt = lax.psum(
        product("btf,fd->btd", mlp_pair[1].activated, full_down[1]).astype(jnp.bfloat16), TP
    ).astype(jnp.float32)
    down_pair = [down_img, down_txt]
    streams = [
        resid_pair[stream_id] + mod_pair[stream_id][:, 5][:, None, :] * down_pair[stream_id]
        for stream_id in range(2)
    ]
    stored = [
        NS(            weights=(full_qkv, full_out, full_up, full_down),
            front=front_pair,
            key_all=key_all,
            value_all=value_all,
            query_all=query_all,
            attended=attended,
            log_total=log_total,
            flat=flat_pair,
            proj=proj_pair,
            mlp=mlp_pair,
            down=down_pair,)
    ]
    grads = [cot_img.astype(jnp.float32), cot_txt.astype(jnp.float32)]
    mod_terms = [None] * layer_count
    gain_terms = [None] * layer_count
    owned_grads = [None] * layer_count
    for layer_id in reversed(range(layer_count)):
        saved = stored[layer_id]
        mod_pair = [own_mod[layer_id, 0], own_mod[layer_id, 1]]
        front_pair = saved.front
        full_qkv, full_out, full_up, full_down = gather_weights(layer_id)
        key_all, value_all = joined_keys(front_pair)
        mlp_parts = [
            mlp_back(
                grads[stream_id],
                mod_pair[stream_id],
                saved.mlp[stream_id],
                saved.down[stream_id],
                full_up[stream_id],
                full_down[stream_id],
            )
            for stream_id in range(2)
        ]
        hidden_img, hidden_txt = (
            lax.psum(mlp_parts[0][3].astype(jnp.bfloat16), TP).astype(jnp.float32),
            lax.psum(mlp_parts[1][3].astype(jnp.bfloat16), TP).astype(jnp.float32),
        )
        hidden_pair = [hidden_img, hidden_txt]
        mlp_norm = [
            norm_branch_back(
                hidden_pair[stream_id],
                saved.mlp[stream_id].normed,
                saved.mlp[stream_id].spread,
                mod_pair[stream_id][:, 4],
                grads[stream_id],
            )
            for stream_id in range(2)
        ]
        attn_parts = [
            attention_branch_back(
                mlp_norm[stream_id][2],
                mod_pair[stream_id],
                saved.proj[stream_id],
                saved.flat[stream_id],
                full_out[stream_id],
            )
            for stream_id in range(2)
        ]
        grad_att = jnp.concatenate(
            [
                attn_parts[0][1].reshape(seq_dev, img_dev, -1, head_dim),
                attn_parts[1][1].reshape(seq_dev, txt_rows, -1, head_dim),
            ],
            axis=1,
        ).astype(jnp.bfloat16)
        query_grad, key_first, key_second, value_first, value_second = attend_back(
            grad_att,
            saved.query_all,
            key_all,
            value_all,
            saved.attended,
            saved.log_total,
            scale_factor,
            img_dev,
        )
        key_img_sum, value_img_sum = (
            lax.psum_scatter(
                key_first[:, :img_total].astype(jnp.bfloat16),
                CTX,
                scatter_dimension=1,
                tiled=True,
            ).astype(jnp.float32),
            lax.psum_scatter(
                value_first[:, :img_total].astype(jnp.bfloat16),
                CTX,
                scatter_dimension=1,
                tiled=True,
            ).astype(jnp.float32),
        )
        key_txt_sum, value_txt_sum = (
            lax.psum(key_first[:, img_total:].astype(jnp.bfloat16), CTX).astype(jnp.float32),
            lax.psum(value_first[:, img_total:].astype(jnp.bfloat16), CTX).astype(jnp.float32),
        )
        key_pair = [
            key_img_sum
            + lax.dynamic_slice_in_dim(key_second[:, :img_total], ctx_start, img_dev, 1),
            key_txt_sum + key_second[:, img_total:],
        ]
        value_pair = [
            value_img_sum
            + lax.dynamic_slice_in_dim(value_second[:, :img_total], ctx_start, img_dev, 1),
            value_txt_sum + value_second[:, img_total:],
        ]
        query_pair = [query_grad[:, :img_dev], query_grad[:, img_dev:]]
        head_parts = [
            head_back(
                query_pair[stream_id],
                key_pair[stream_id],
                value_pair[stream_id],
                front_pair[stream_id],
                norm_gain[layer_id, stream_id],
            )
            for stream_id in range(2)
        ]
        input_img, input_txt = (
            lax.psum(
                product("btkc,dkc->btd", head_parts[0][1], full_qkv[0]).astype(jnp.bfloat16), TP
            ).astype(jnp.float32),
            lax.psum(
                product("btkc,dkc->btd", head_parts[1][1], full_qkv[1]).astype(jnp.bfloat16), TP
            ).astype(jnp.float32),
        )
        input_pair = [input_img, input_txt]
        attn_norm = [
            norm_branch_back(
                input_pair[stream_id],
                front_pair[stream_id].normed,
                front_pair[stream_id].spread,
                mod_pair[stream_id][:, 1],
                mlp_norm[stream_id][2],
            )
            for stream_id in range(2)
        ]
        grads = [attn_norm[stream_id][2] for stream_id in range(2)]
        mod_rows = [
            jnp.stack(
                [
                    attn_norm[stream_id][0],
                    attn_norm[stream_id][1],
                    attn_parts[stream_id][0],
                    mlp_norm[stream_id][0],
                    mlp_norm[stream_id][1],
                    mlp_parts[stream_id][0],
                ],
                axis=1,
            )
            for stream_id in range(2)
        ]
        mod_terms[layer_id] = jnp.stack([mod_rows[0], mod_rows[1] / ctx_count]) / tp_count
        gain_terms[layer_id] = jnp.stack([head_parts[0][0], head_parts[1][0] / ctx_count])
        qkv_stack = jnp.stack(
            [
                product("btd,btkc->dkc", front_pair[stream_id].hidden, head_parts[stream_id][1])
                for stream_id in range(2)
            ]
        )
        out_stack = jnp.stack([attn_parts[stream_id][2] for stream_id in range(2)])
        up_stack = jnp.stack([mlp_parts[stream_id][2] for stream_id in range(2)])
        down_stack = jnp.stack([mlp_parts[stream_id][1] for stream_id in range(2)])
        qkv_term = jnp.concatenate([qkv_stack[0:1], qkv_stack[1:2] / ctx_count])
        out_term = jnp.concatenate([out_stack[0:1], out_stack[1:2] / ctx_count])
        up_term = jnp.concatenate([up_stack[0:1], up_stack[1:2] / ctx_count])
        down_term = jnp.concatenate([down_stack[0:1], down_stack[1:2] / ctx_count])
        owned = (
            lax.psum_scatter(
                qkv_term.astype(jnp.bfloat16), ROWS, scatter_dimension=1, tiled=True
            ).astype(jnp.float32),
            lax.psum_scatter(
                out_term.astype(jnp.bfloat16), ROWS, scatter_dimension=2, tiled=True
            ).astype(jnp.float32),
            lax.psum_scatter(
                up_term.astype(jnp.bfloat16), ROWS, scatter_dimension=1, tiled=True
            ).astype(jnp.float32),
            lax.psum_scatter(
                down_term.astype(jnp.bfloat16), ROWS, scatter_dimension=2, tiled=True
            ).astype(jnp.float32),
        )
        owned_grads[layer_id] = owned
    mod_local = jnp.stack(mod_terms)
    mod_zero = jnp.zeros(
        (layer_count, 2, seq_dev * lax.axis_size(DP)) + mod_local.shape[3:], jnp.float32
    )
    mod_term = lax.dynamic_update_slice_in_dim(mod_zero, mod_local, seq_start, 2)
    mod_full, gain_grad = lax.psum((mod_term, jnp.stack(gain_terms)), ALL)
    mod_grad = jnp.einsum(
        "sm,ltskc->ltmkc", cond_act.astype(jnp.float32), mod_full, precision=lax.Precision.HIGHEST
    )
    qkv_grad = jnp.stack([owned_grads[0][0]])
    out_grad = jnp.stack([owned_grads[0][1]])
    up_grad = jnp.stack([owned_grads[0][2]])
    down_grad = jnp.stack([owned_grads[0][3]])
    mod_next, mod_moment_next, mod_second_next = adam_step(
        mod_weight, mod_moment, mod_second, mod_grad
    )
    qkv_next, qkv_moment_next, qkv_second_next = adam_step(
        qkv_weight, qkv_moment, qkv_second, qkv_grad
    )
    out_next, out_moment_next, out_second_next = adam_step(
        out_weight, out_moment, out_second, out_grad
    )
    up_next, up_moment_next, up_second_next = adam_step(up_weight, up_moment, up_second, up_grad)
    down_next, down_moment_next, down_second_next = adam_step(
        down_weight, down_moment, down_second, down_grad
    )
    gain_next, gain_moment_next, gain_second_next = adam_step(
        norm_gain, gain_moment, gain_second, gain_grad
    )
    return (
        streams[0].astype(jnp.bfloat16),
        streams[1].astype(jnp.bfloat16),
        grads[0].astype(jnp.bfloat16),
        grads[1].astype(jnp.bfloat16),
        mod_grad,
        mod_next,
        mod_moment_next,
        mod_second_next,
        qkv_grad,
        qkv_next,
        qkv_moment_next,
        qkv_second_next,
        out_grad,
        out_next,
        out_moment_next,
        out_second_next,
        up_grad,
        up_next,
        up_moment_next,
        up_second_next,
        down_grad,
        down_next,
        down_moment_next,
        down_second_next,
        gain_grad,
        gain_next,
        gain_moment_next,
        gain_second_next,
    )


class Place:
    def __init__(self, zn):
        self.zn = zn
        self.d, self.c, self.t = lax.axis_index(DP), lax.axis_index(CTX), lax.axis_index(TP)
        self.y, self.k = self.d // 2, self.d % 2
        self.d_core = self.y * 2 + (1 - self.k)
        self.d_y = (1 - self.y) * 2 + self.k
        self.t_x = 1 - self.t

    def ahead(self, step):
        return (self.c + step) % self.zn

    def behind(self, step):
        return (self.c + self.zn - step) % self.zn

    def greet(self, core=True, y=True, x=True, z=True):
        sem = pltpu.get_barrier_semaphore()
        count = 0
        for wanted, where in ((x, {TP: self.t_x}), (core, {DP: self.d_core}), (y, {DP: self.d_y})):
            if wanted:
                pl.semaphore_signal(sem, inc=1, device_id=where, device_id_type=pl.DeviceIdType.MESH)
                count += 1
        if z:
            for step in range(1, self.zn):
                pl.semaphore_signal(
                    sem, inc=1, device_id={CTX: self.ahead(step)}, device_id_type=pl.DeviceIdType.MESH
                )
                count += 1
        pl.semaphore_wait(sem, count)


def remote(src, dst, send, recv, where):
    copy = pltpu.make_async_remote_copy(
        src_ref=src,
        dst_ref=dst,
        send_sem=send,
        recv_sem=recv,
        device_id=where,
        device_id_type=pl.DeviceIdType.MESH,
    )
    copy.start()
    return copy


def local(src, dst, sem):
    copy = pltpu.make_async_copy(src, dst, sem)
    copy.start()
    return copy


HBM = pl.BlockSpec(memory_space=pl.ANY)
VMEM = pl.BlockSpec(memory_space=pltpu.VMEM)
DMA = pltpu.SemaphoreType.DMA


def call(kernel, ident, ins, outs, scratch, args, flops=0):
    return pl.pallas_call(
        kernel,
        out_shape=[shape for shape, _ in outs],
        in_specs=ins,
        out_specs=[spec for _, spec in outs],
        scratch_shapes=scratch,
        compiler_params=pltpu.CompilerParams(
            collective_id=ident, has_side_effects=True, vmem_limit_bytes=60 * 1024 * 1024
        ),
    )(*args)


def shaped(shape, dtype):
    return jax.ShapeDtypeStruct(shape, dtype)


def spread_kernel(
    zn, wa, wu, wd, xi, ci, mp, ga, gu, gd, xo, co, mod,
    bw, bx, my, m2, mc, m1, mx, slots,
    zs, zr, ys, yr, cs, cr, xs, xr, ms, mr, loc,
):
    me = Place(zn)
    me.greet()
    d, c, t, y, k = me.d, me.c, me.t, me.y, me.k
    outs = (ga, gu, gd)
    own = []
    bounce = []
    for kind, w in enumerate((wa, wu, wd)):
        bounce.append(local(w.at[c], bw.at[kind], loc.at[kind]))
    for act, a in enumerate((xi, ci)):
        bounce.append(local(a, bx.at[act], loc.at[3 + act]))
    pending = []
    m_y = remote(mp.at[pl.ds((1 - y) * 2, 2)], my, ms.at[0], mr.at[0], {DP: me.d_y})
    zcopies = {}

    def send_tokens(act, a, o):
        zcopies[6 + act] = [
            remote(a.at[t], o.at[c, t], zs.at[6 + act, s - 1], zr.at[6 + act, s - 1], {CTX: me.ahead(s)})
            for s in range(1, zn)
        ]

    def send_weights(kind, w):
        for st in range(2):
            zcopies[kind * 2 + st] = [
                remote(
                    w.at[me.ahead(s), st],
                    outs[kind].at[st, d * zn + c],
                    zs.at[kind * 2 + st, s - 1],
                    zr.at[kind * 2 + st, s - 1],
                    {CTX: me.ahead(s)},
                )
                for s in range(1, zn)
            ]

    send_tokens(0, xi, xo)
    send_weights(0, wa)
    send_weights(1, wu)
    send_weights(2, wd)
    send_tokens(1, ci, co)

    for kind in range(3):
        bounce[kind].wait()
        for st in range(2):
            own.append(local(bw.at[kind, st], outs[kind].at[st, d * zn + c], loc.at[5 + kind * 2 + st]))
    for act, o in enumerate((xo, co)):
        bounce[3 + act].wait()
        own.append(local(bx.at[act], o.at[c], loc.at[11 + act]))

    m_y.wait()
    m2[...] = mp[pl.ds(y * 2, 2)] + my[...]
    m_c = remote(m2.at[1 - k], mc, ms.at[1], mr.at[1], {DP: me.d_core})
    m_c.wait()
    m1[...] = m2[k] + mc[...]
    m_x = remote(m1, mx, ms.at[2], mr.at[2], {TP: me.t_x})
    m_x.wait()
    slots[c] = m1[...] + mx[...]
    m_z = [
        remote(slots.at[c], slots.at[c], ms.at[2 + s], mr.at[2 + s], {CTX: me.ahead(s)})
        for s in range(1, zn)
    ]

    def forward_tokens(act, o):
        for s in range(1, zn):
            zcopies[6 + act][s - 1].wait()
            src = me.behind(s)
            pending.append(
                remote(o.at[src, t], o.at[src, t], xs.at[act, s - 1], xr.at[act, s - 1], {TP: me.t_x})
            )

    forward_tokens(0, xo)
    ycopies = []
    for chunk in range(6):
        kind, st = divmod(chunk, 2)
        g = outs[kind]
        for copy in zcopies[chunk]:
            copy.wait()
        own[chunk].wait()
        mine = g.at[st, pl.ds(d * zn, zn)]
        ycopies.append(remote(mine, mine, ys.at[chunk], yr.at[chunk], {DP: me.d_y}))
        pending.append(remote(mine, mine, cs.at[chunk, 0], cr.at[chunk, 0], {DP: me.d_core}))
        if chunk:
            pass_on(me, outs, chunk - 1, ycopies, pending, cs, cr)
        if chunk == 1:
            for copy in m_z:
                copy.wait()
            total = slots[0]
            for z in range(1, zn):
                total = total + slots[z]
            mod[...] = total
    forward_tokens(1, co)
    pass_on(me, outs, 5, ycopies, pending, cs, cr)
    for copy in pending:
        copy.wait()
    for copy in own[6:]:
        copy.wait()


def pass_on(me, outs, chunk, ycopies, pending, cs, cr):
    kind, st = divmod(chunk, 2)
    ycopies[chunk].wait()
    there = outs[kind].at[st, pl.ds(me.d_y * me.zn, me.zn)]
    pending.append(remote(there, there, cs.at[chunk, 1], cr.at[chunk, 1], {DP: me.d_core}))


def spread(zn, wa, wu, wd, xi, ci, mp):
    rows, width = wa.shape[2:]
    half, dim = xi.shape[1:]
    lines = mp.shape[1]
    weight = shaped((2, 4 * zn, rows, width), BF)
    token = shaped((zn, 2, half, dim), BF)
    return call(
        functools.partial(spread_kernel, zn),
        0,
        [HBM] * 5 + [VMEM],
        [(weight, HBM)] * 3 + [(token, HBM)] * 2 + [(shaped((lines, 128), F32), VMEM)],
        [
            pltpu.VMEM((3, 2, rows, width), BF),
            pltpu.VMEM((2, 2, half, dim), BF),
            pltpu.VMEM((2, lines, 128), F32),
            pltpu.VMEM((2, lines, 128), F32),
            pltpu.VMEM((lines, 128), F32),
            pltpu.VMEM((lines, 128), F32),
            pltpu.VMEM((lines, 128), F32),
            pltpu.VMEM((zn, lines, 128), F32),
            DMA((8, zn)), DMA((8, zn)), DMA((6,)), DMA((6,)), DMA((6, 2)), DMA((6, 2)),
            DMA((2, zn)), DMA((2, zn)), DMA((2 + zn,)), DMA((2 + zn,)), DMA((13,)),
        ],
        (wa, wu, wd, xi, ci, mp),
    )


CHUNK = 16


def sum_start(me, arrays, own, recvx, xs, xr, loc):
    order = list(range(1, me.zn)) + [0]
    copies = {}
    for a, parts in enumerate(arrays):
        for s in order:
            zb = me.ahead(s)
            at = 0
            group = []
            for p, part in enumerate(parts):
                n = part.shape[2]
                group.append(
                    remote(
                        part.at[zb, me.t_x],
                        recvx.at[a, s, pl.ds(at, n)],
                        xs.at[a, s, p],
                        xr.at[a, s, p],
                        {TP: me.t_x},
                    )
                )
                group.append(local(part.at[zb, me.t], own.at[a, s, pl.ds(at, n)], loc.at[a, s, p]))
                at += n
            copies[a, s] = group
    return copies


def sum_x(me, a, copies, own, recvx, sumb, recvz, total, zs, zr):
    rows = own.shape[2]
    out = []
    for s in list(range(1, me.zn)) + [0]:
        for copy in copies[a, s]:
            copy.wait()
        if s:

            @pl.loop(0, rows // CHUNK)
            def _(i):
                at = pl.ds(pl.multiple_of(i * CHUNK, CHUNK), CHUNK)
                sumb[a, s, at] = (own[a, s, at].astype(F32) + recvx[a, s, at].astype(F32)).astype(BF)

            out.append(
                remote(sumb.at[a, s], recvz.at[a, s], zs.at[a, s], zr.at[a, s], {CTX: me.ahead(s)})
            )
        else:

            @pl.loop(0, rows // CHUNK)
            def _(i):
                at = pl.ds(pl.multiple_of(i * CHUNK, CHUNK), CHUNK)
                total[a, at] = own[a, s, at].astype(F32) + recvx[a, s, at].astype(F32)

    return out


def sum_z(me, a, copies, recvz, total):
    for copy in copies:
        copy.wait()
    rows = total.shape[1]

    @pl.loop(0, rows // CHUNK)
    def _(i):
        at = pl.ds(pl.multiple_of(i * CHUNK, CHUNK), CHUNK)
        value = total[a, at]
        for s in range(1, me.zn):
            value = value + recvz[a, s, at].astype(F32)
        total[a, at] = value


def share_start(me, block, outs, sizes, zs, zr, xs, xr, loc):
    copies = []
    at = 0
    for p, (o, n) in enumerate(zip(outs, sizes)):
        src = block.at[pl.ds(at, n)]
        at += n
        dst = o.at[me.c, me.t]
        group = [
            remote(src, dst, zs.at[p, s], zr.at[p, s], {CTX: me.ahead(s)}) for s in range(1, me.zn)
        ]
        group.append(remote(src, dst, xs.at[p, 0], xr.at[p, 0], {TP: me.t_x}))
        group.append(local(src, dst, loc.at[p]))
        copies.append(group)
    return copies


def share_end(me, copies, outs, xs, xr):
    passed = []
    for s in range(1, me.zn):
        src = me.behind(s)
        for p, o in enumerate(outs):
            copies[p][s - 1].wait()
            passed.append(
                remote(o.at[src, me.t], o.at[src, me.t], xs.at[p, s], xr.at[p, s], {TP: me.t_x})
            )
    for group in copies:
        for copy in group[me.zn - 1 :]:
            copy.wait()
    for copy in passed:
        copy.wait()


def row_loops(sizes, fn):
    at = 0
    for stream, n in enumerate(sizes):

        @pl.loop(0, n // CHUNK)
        def _(i, at=at, stream=stream):
            fn(stream, pl.ds(pl.multiple_of(at + i * CHUNK, CHUNK), CHUNK))

        at += n


def line(mod, stream, which):
    return mod[stream * 6 + which][None, :]


def sum_scratch(count, zn, rows, dim):
    return [
        pltpu.VMEM((count, zn, rows, dim), BF),
        pltpu.VMEM((count, zn, rows, dim), BF),
        pltpu.VMEM((count, zn, rows, dim), BF),
        pltpu.VMEM((count, zn, rows, dim), BF),
        pltpu.VMEM((count, rows, dim), F32),
        DMA((count, zn, 2)), DMA((count, zn, 2)), DMA((count, zn, 2)),
        DMA((count, zn)), DMA((count, zn)),
    ]


def share_scratch(zn, rows, dim):
    return [
        pltpu.VMEM((rows, dim), BF),
        DMA((2, zn)), DMA((2, zn)), DMA((2, zn)), DMA((2, zn)), DMA((2,)),
    ]


def middle_kernel(
    zn, sizes, pi, pt, xr_rows, mod, hi, ht, resid, proj,
    own, recvx, sumb, recvz, total, sxs, sxr, sloc, szs, szr,
    hb, gzs, gzr, gxs, gxr, gloc,
):
    me = Place(zn)
    me.greet(core=False, y=False)
    copies = sum_start(me, [(pi, pt)], own, recvx, sxs, sxr, sloc)
    zc = sum_x(me, 0, copies, own, recvx, sumb, recvz, total, szs, szr)
    sum_z(me, 0, zc, recvz, total)

    def rows(stream, at):
        p = total[0, at]
        proj[at] = p
        value = xr_rows[at].astype(F32) + line(mod, stream, 2) * p
        resid[at] = value
        normed, _ = layer_norm(value)
        hb[at] = (normed * (1.0 + line(mod, stream, 4)) + line(mod, stream, 3)).astype(BF)

    row_loops(sizes, rows)
    copies = share_start(me, hb, (hi, ht), sizes, gzs, gzr, gxs, gxr, gloc)
    share_end(me, copies, (hi, ht), gxs, gxr)


def middle(zn, sizes, pi, pt, rows, mod):
    dim = rows.shape[1]
    total = sum(sizes)
    return call(
        functools.partial(middle_kernel, zn, sizes),
        1,
        [HBM, HBM, VMEM, VMEM],
        [
            (shaped(pi.shape, BF), HBM),
            (shaped(pt.shape, BF), HBM),
            (shaped((total, dim), F32), VMEM),
            (shaped((total, dim), F32), VMEM),
        ],
        sum_scratch(1, zn, total, dim) + share_scratch(zn, total, dim),
        (pi, pt, rows, mod),
    )


def turn_kernel(
    zn, sizes, hi, ht, mi, mt, resid, proj, cot, mod, bi, bt, out, rgrad, sums,
    own, recvx, sumb, recvz, total, sxs, sxr, sloc, szs, szr,
    bb, gzs, gzr, gxs, gxr, gloc,
):
    me = Place(zn)
    me.greet(core=False, y=False)
    copies = sum_start(me, [(hi, ht), (mi, mt)], own, recvx, sxs, sxr, sloc)
    zh = sum_x(me, 0, copies, own, recvx, sumb, recvz, total, szs, szr)
    sums[...] = jnp.zeros_like(sums)
    sum_z(me, 0, zh, recvz, total)

    def rows(stream, at):
        h = total[0, at]
        normed, spread_ = layer_norm(resid[at])
        g = cot[at].astype(F32)
        value = g + norm_back(h * (1.0 + line(mod, stream, 4)), normed, spread_)
        rgrad[at] = value
        bb[at] = (value * line(mod, stream, 2)).astype(BF)
        sums[stream, 0] += jnp.sum(value * proj[at], axis=0)
        sums[stream, 1] += jnp.sum(h, axis=0)
        sums[stream, 2] += jnp.sum(h * normed, axis=0)

    row_loops(sizes, rows)
    shared = share_start(me, bb, (bi, bt), sizes, gzs, gzr, gxs, gxr, gloc)
    zm = sum_x(me, 1, copies, own, recvx, sumb, recvz, total, szs, szr)
    share_end(me, shared, (bi, bt), gxs, gxr)
    sum_z(me, 1, zm, recvz, total)

    def tail(stream, at):
        m = total[1, at]
        out[at] = (resid[at] + line(mod, stream, 5) * m).astype(BF)
        sums[stream, 3] += jnp.sum(cot[at].astype(F32) * m, axis=0)

    row_loops(sizes, tail)


def turn(zn, sizes, hi, ht, mi, mt, resid, proj, cot, mod):
    total, dim = resid.shape
    return call(
        functools.partial(turn_kernel, zn, sizes),
        2,
        [HBM] * 4 + [VMEM] * 4,
        [
            (shaped(hi.shape, BF), HBM),
            (shaped(ht.shape, BF), HBM),
            (shaped((total, dim), BF), VMEM),
            (shaped((total, dim), F32), VMEM),
            (shaped((2, 4, dim), F32), VMEM),
        ],
        sum_scratch(2, zn, total, dim) + share_scratch(zn, total, dim),
        (hi, ht, mi, mt, resid, proj, cot, mod),
    )


def finish_kernel(
    zn, sizes, ai, at_, x_rows, rgrad, out, sums, gains, mod, oi, ot, gsum,
    own, recvx, sumb, recvz, total, sxs, sxr, sloc, szs, szr,
    ob, msum, mx, slots, xs, xr, zs, zr, fs, fr, loc, ms, mr,
):
    me = Place(zn)
    me.greet()
    c, t = me.c, me.t
    n_img, n_txt = sizes
    copies = sum_start(me, [(ai, at_)], own, recvx, sxs, sxr, sloc)

    def keep(stream, at):
        ob[0, at] = out[at]

    row_loops(sizes, keep)
    zc = sum_x(me, 0, copies, own, recvx, sumb, recvz, total, szs, szr)
    msum[...] = jnp.zeros_like(msum)
    sum_z(me, 0, zc, recvz, total)

    def rows(stream, at):
        h = total[0, at]
        normed, spread_ = layer_norm(x_rows[at].astype(F32))
        value = rgrad[at] + norm_back(h * (1.0 + line(mod, stream, 1)), normed, spread_)
        ob[1, at] = value.astype(BF)
        msum[stream * 6] += jnp.sum(h, axis=0)
        msum[stream * 6 + 1] += jnp.sum(h * normed, axis=0)

    row_loops(sizes, rows)
    for stream in range(2):
        for which in range(4):
            msum[stream * 6 + 2 + which] = sums[stream, which]
    msum[12] = gains[0]
    m_x = remote(msum, mx, ms.at[0], mr.at[0], {TP: me.t_x})
    img = ob.at[:, pl.ds(0, n_img)]
    txt = ob.at[:, pl.ds(n_img, n_txt)]
    done = [
        remote(img, oi.at[:, t], xs.at[0], xr.at[0], {TP: me.t_x}),
        remote(txt, ot.at[:, c, t], xs.at[1], xr.at[1], {TP: me.t_x}),
        local(img, oi.at[:, t], loc.at[0]),
        local(txt, ot.at[:, c, t], loc.at[1]),
    ]
    over_z = [
        remote(txt, ot.at[:, c, t], zs.at[s], zr.at[s], {CTX: me.ahead(s)}) for s in range(1, zn)
    ]
    m_x.wait()
    slots[c] = msum[...] + mx[...]
    m_z = [
        remote(slots.at[c], slots.at[c], ms.at[s], mr.at[s], {CTX: me.ahead(s)}) for s in range(1, zn)
    ]
    for s in range(1, zn):
        over_z[s - 1].wait()
        src = me.behind(s)
        done.append(
            remote(ot.at[:, src, t], ot.at[:, src, t], fs.at[s], fr.at[s], {TP: me.t_x})
        )
    for copy in m_z:
        copy.wait()
    value = slots[0]
    for z in range(1, zn):
        value = value + slots[z]
    gsum[me.d] = value
    m_c = remote(gsum.at[me.d], gsum.at[me.d], ms.at[zn], mr.at[zn], {DP: me.d_core})
    m_c.wait()
    pair = gsum.at[pl.ds(me.y * 2, 2)]
    m_y = remote(pair, pair, ms.at[zn + 1], mr.at[zn + 1], {DP: me.d_y})
    m_y.wait()
    for copy in done:
        copy.wait()


def finish(zn, sizes, ai, at_, x_rows, rgrad, out, sums, gains, mod):
    total, dim = rgrad.shape
    n_img, n_txt = sizes
    return call(
        functools.partial(finish_kernel, zn, sizes),
        3,
        [HBM] * 2 + [VMEM] * 6,
        [
            (shaped((2, 2, n_img, dim), BF), HBM),
            (shaped((2, zn, 2, n_txt, dim), BF), HBM),
            (shaped((4, 16, dim), F32), VMEM),
        ],
        sum_scratch(1, zn, total, dim)
        + [
            pltpu.VMEM((2, total, dim), BF),
            pltpu.VMEM((16, dim), F32),
            pltpu.VMEM((16, dim), F32),
            pltpu.VMEM((zn, 16, dim), F32),
            DMA((2,)), DMA((2,)), DMA((zn,)), DMA((zn,)), DMA((zn,)), DMA((zn,)), DMA((2,)),
            DMA((zn + 2,)), DMA((zn + 2,)),
        ],
        (ai, at_, x_rows, rgrad, out, sums, gains, mod),
    )


def return_kernel(
    zn, da, du, dd, ra, ru, rd, own, crecv, part, yrecv,
    loc, cs, cr, ys, yr, zs, zr, ls,
):
    me = Place(zn)
    me.greet()
    y, k = me.y, me.k
    c = me.c
    grads, outs = (da, du, dd), (ra, ru, rd)
    order = [5, 4, 3, 2, 1, 0]
    rows = own.shape[3]
    first = {}
    for chunk in order:
        kind, st = divmod(chunk, 2)
        g = grads[kind]
        group = []
        for j, yy in enumerate((1 - y, y)):
            theirs = g.at[st, pl.ds((yy * 2 + 1 - k) * zn, zn)]
            mine = g.at[st, pl.ds((yy * 2 + k) * zn, zn)]
            group.append(
                (
                    remote(theirs, crecv.at[chunk, j], cs.at[chunk, j], cr.at[chunk, j], {DP: me.d_core}),
                    local(mine, own.at[chunk, j], loc.at[chunk, j]),
                )
            )
        first[chunk] = group
    second = {}

    def add(dst, one, two):
        @pl.loop(0, zn)
        def _(z):
            @pl.loop(0, rows // CHUNK)
            def _(i):
                at = pl.ds(pl.multiple_of(i * CHUNK, CHUNK), CHUNK)
                dst[z, at] = (one[z, at].astype(F32) + two[z, at].astype(F32)).astype(BF)

    for chunk in order:
        for j in range(2):
            for copy in first[chunk][j]:
                copy.wait()
            add(part.at[chunk, j], own.at[chunk, j], crecv.at[chunk, j])
            if j == 0:
                second[chunk] = remote(
                    part.at[chunk, 0], yrecv.at[chunk], ys.at[chunk], yr.at[chunk], {DP: me.d_y}
                )
    last = []
    for chunk in order:
        kind, st = divmod(chunk, 2)
        second[chunk].wait()
        add(own.at[chunk, 0], part.at[chunk, 1], yrecv.at[chunk])
        for s in range(1, zn):
            last.append(
                remote(
                    own.at[chunk, 0, me.ahead(s)],
                    outs[kind].at[c, st],
                    zs.at[chunk, s],
                    zr.at[chunk, s],
                    {CTX: me.ahead(s)},
                )
            )
        last.append(local(own.at[chunk, 0, c], outs[kind].at[c, st], ls.at[chunk]))
    for copy in last:
        copy.wait()


def give_back(zn, da, du, dd):
    rows, width = da.shape[2:]
    shape = shaped((zn, 2, rows, width), BF)
    return call(
        functools.partial(return_kernel, zn),
        4,
        [HBM] * 3,
        [(shape, HBM)] * 3,
        [
            pltpu.VMEM((6, 2, zn, rows, width), BF),
            pltpu.VMEM((6, 2, zn, rows, width), BF),
            pltpu.VMEM((6, 2, zn, rows, width), BF),
            pltpu.VMEM((6, zn, rows, width), BF),
            DMA((6, 2)), DMA((6, 2)), DMA((6, 2)), DMA((6,)), DMA((6,)),
            DMA((6, zn)), DMA((6, zn)), DMA((6,)),
        ],
        (da, du, dd),
    )


def dot(one, two, dims):
    return lax.dot_general(one, two, ((dims[:1], dims[1:]), ((), ())), preferred_element_type=F32)


def split_body(
    img_in, txt_in, cond, mod_weight, qkv_weight, out_weight, up_weight, down_weight, norm_gain,
    cot_img, cot_txt, mod_moment, qkv_moment, out_moment, up_moment, down_moment, gain_moment,
    mod_second, qkv_second, out_second, up_second, down_second, gain_second,
):
    zn = lax.axis_size(CTX)
    dim = img_in.shape[2]
    img_dev, txt_len = img_in.shape[1], txt_in.shape[1]
    n_img = img_dev // 2
    n_txt = -(-txt_len // (2 * zn * CHUNK)) * CHUNK
    sizes = (n_img, n_txt)
    txt_pad = n_txt * 2 * zn
    img_all = img_dev * zn
    head_dim = norm_gain.shape[-1]
    rows = qkv_weight.shape[2]
    col = qkv_weight.shape[4] // zn
    heads = col // head_dim
    ff = up_weight.shape[3] // zn
    scale_factor = head_dim ** (-0.5)
    c, t = lax.axis_index(CTX), lax.axis_index(TP)
    seq = lax.axis_index(DP)
    n_seq = lax.axis_size(DP)

    cond_act = jax.nn.silu(cond.astype(F32)).astype(BF)
    mod_part = product("sm,tmkc->stkc", cond_act, mod_weight[0].astype(BF))
    mod_part = mod_part.reshape(n_seq, -1, 128)

    qkv_low = qkv_weight[0].astype(BF).reshape(2, rows, 3, zn, col)
    qkv_low = jnp.transpose(qkv_low, (3, 0, 1, 2, 4)).reshape(zn, 2, rows, 3 * col)
    out_low = jnp.transpose(out_weight[0].astype(BF).reshape(2, zn, col, rows), (1, 0, 3, 2))
    wa = jnp.concatenate([qkv_low, out_low], axis=3)
    wu = jnp.transpose(up_weight[0].astype(BF).reshape(2, rows, zn, ff), (2, 0, 1, 3))
    wd = jnp.transpose(down_weight[0].astype(BF).reshape(2, zn, ff, rows), (1, 0, 3, 2))

    cot_rows_txt = jnp.pad(cot_txt[0], ((0, txt_pad - txt_len), (0, 0)))
    txt_rows = jnp.pad(txt_in[0], ((0, txt_pad - txt_len), (0, 0)))
    ga, gu, gd, xo, co, mod = spread(
        zn, wa, wu, wd, img_in.reshape(2, n_img, dim), cot_img.reshape(2, n_img, dim), mod_part
    )
    wide = 3 * col + col
    ga = ga.reshape(2, -1, wide)
    gu = gu.reshape(2, -1, ff)
    gd = gd.reshape(2, -1, ff)
    qkv_full = [ga[st, :, : 3 * col] for st in range(2)]
    out_full = [ga[st, :, 3 * col :] for st in range(2)]
    mod = mod.reshape(12, dim)
    mods = [[mod[st * 6 + which][None, :] for which in range(6)] for st in range(2)]

    def own_rows(img, txt):
        one = lax.dynamic_slice_in_dim(img, t * n_img, n_img, 0)
        two = lax.dynamic_slice_in_dim(txt, (c * 2 + t) * n_txt, n_txt, 0)
        return jnp.concatenate([one, two], axis=0)

    x_rows = own_rows(img_in[0], txt_rows)
    cot_rows = own_rows(cot_img[0], cot_rows_txt)
    tokens = [xo.reshape(img_all, dim), txt_rows]
    cots = [co.reshape(img_all, dim), cot_rows_txt]

    hidden, packed = [], []
    for st in range(2):
        normed, _ = layer_norm(tokens[st].astype(F32))
        hidden.append((normed * (1.0 + mods[st][1]) + mods[st][0]).astype(BF))
        packed.append(dot(hidden[st], qkv_full[st], (1, 0)))
    lengths = (img_all, txt_pad)
    packs = [p.reshape(n, 3, heads, head_dim) for p, n in zip(packed, lengths)]
    q_norm = [rms_norm(p[:, 0]) for p in packs]
    k_norm = [rms_norm(p[:, 1]) for p in packs]
    gains = norm_gain[0]

    def by_head(pair):
        return jnp.transpose(jnp.concatenate(pair, axis=0), (1, 0, 2))

    queries = by_head([(q_norm[st][0] * gains[st, 0]).astype(BF) for st in range(2)])
    keys = by_head([(k_norm[st][0] * gains[st, 1]).astype(BF) for st in range(2)])
    values = by_head([packs[st][:, 2].astype(BF) for st in range(2)])
    live = jnp.arange(img_all + txt_pad) < img_all + txt_len
    scores = product("hqd,hkd->hqk", queries, keys) * scale_factor
    scores = jnp.where(live[None, None, :], scores, -1e30)
    peak = jnp.max(scores, axis=-1, keepdims=True)
    log_total = peak + jnp.log(jnp.sum(jnp.exp(scores - peak), axis=-1, keepdims=True))
    probs = jnp.exp(scores - log_total)
    probs_low = probs.astype(BF)
    attended = product("hqk,hkd->hqd", probs_low, values)
    flat = jnp.transpose(attended.astype(BF), (1, 0, 2)).reshape(-1, col)
    flats = [flat[:img_all], flat[img_all:]]

    def blocks(img, txt):
        return img.reshape(zn, 2, n_img, dim), txt.reshape(zn, 2, n_txt, dim)

    proj = [dot(flats[st], out_full[st], (1, 1)).astype(BF) for st in range(2)]
    hi, ht, resid, proj_rows = middle(zn, sizes, *blocks(*proj), x_rows, mod)

    hidden_m = [hi.reshape(img_all, dim), ht.reshape(txt_pad, dim)]
    mlp_out, mlp_in, du, dd = [], [], [], []
    for st in range(2):
        pre_act = dot(hidden_m[st], gu[st], (1, 0))
        activated, pull = jax.vjp(gelu_tanh, pre_act)
        activated = activated.astype(BF)
        mlp_out.append(dot(activated, gd[st], (1, 1)).astype(BF))
        branch = (cots[st].astype(F32) * mods[st][5]).astype(BF)
        pre_grad = pull(dot(branch, gd[st], (1, 0)))[0].astype(BF)
        mlp_in.append(dot(pre_grad, gu[st], (1, 1)).astype(BF))
        dd.append(dot(branch, activated, (0, 0)).astype(BF))
        du.append(dot(hidden_m[st], pre_grad, (0, 0)).astype(BF))
    bi, bt, out_rows, rgrad, sums = turn(
        zn, sizes, *blocks(*mlp_in), *blocks(*mlp_out), resid, proj_rows, cot_rows, mod
    )

    branch_a = [bi.reshape(img_all, dim), bt.reshape(txt_pad, dim)]
    att_grad = jnp.concatenate([dot(branch_a[st], out_full[st], (1, 0)) for st in range(2)], axis=0)
    att_grad = jnp.transpose(att_grad.astype(BF).reshape(-1, heads, head_dim), (1, 0, 2))
    delta = jnp.sum(att_grad.astype(F32) * attended, axis=-1, keepdims=True)
    prob_grad = product("hqd,hkd->hqk", att_grad, values)
    score_grad = (probs * (prob_grad - delta) * scale_factor).astype(BF)
    query_grad = jnp.transpose(product("hqk,hkd->hqd", score_grad, keys), (1, 0, 2))
    key_grad = jnp.transpose(product("hqk,hqd->hkd", score_grad, queries), (1, 0, 2))
    value_grad = jnp.transpose(product("hqk,hqd->hkd", probs_low, att_grad), (1, 0, 2))
    gain_lines, input_part, da = [], [], []
    for st in range(2):
        part = slice(0, img_all) if st == 0 else slice(img_all, None)
        q_grad, k_grad = query_grad[part], key_grad[part]
        gain_lines.append(jnp.sum(q_grad * q_norm[st][0], axis=(0, 1)))
        gain_lines.append(jnp.sum(k_grad * k_norm[st][0], axis=(0, 1)))
        q_raw = rms_back(q_grad * gains[st, 0], *q_norm[st])
        k_raw = rms_back(k_grad * gains[st, 1], *k_norm[st])
        packed_grad = jnp.stack([q_raw, k_raw, value_grad[part]], axis=1)
        packed_grad = packed_grad.reshape(-1, 3 * col).astype(BF)
        input_part.append(dot(packed_grad, qkv_full[st], (1, 1)).astype(BF))
        d_qkv = dot(hidden[st], packed_grad, (0, 0)).astype(BF)
        d_out = dot(branch_a[st], flats[st], (0, 0)).astype(BF)
        da.append(jnp.concatenate([d_qkv, d_out], axis=1))
    gain_row = jnp.pad(jnp.concatenate(gain_lines), (0, dim - 4 * head_dim))[None, :]
    oi, ot, gsum = finish(zn, sizes, *blocks(*input_part), x_rows, rgrad, out_rows, sums, gain_row, mod)
    img_out, img_grad = oi[0].reshape(1, img_dev, dim), oi[1].reshape(1, img_dev, dim)
    txt_out = ot[0].reshape(1, txt_pad, dim)[:, :txt_len]
    txt_grad = ot[1].reshape(1, txt_pad, dim)[:, :txt_len]

    def stacked(pair):
        return jnp.stack(pair).reshape(2, n_seq * zn, rows, -1)

    ra, ru, rd = give_back(zn, stacked(da), stacked(du), stacked(dd))
    qkv_grad = ra[..., : 3 * col].reshape(zn, 2, rows, 3, col)
    qkv_grad = jnp.transpose(qkv_grad, (1, 2, 3, 0, 4)).reshape(qkv_weight.shape).astype(F32)
    out_grad = jnp.transpose(ra[..., 3 * col :], (1, 0, 3, 2)).reshape(out_weight.shape).astype(F32)
    up_grad = jnp.transpose(ru, (1, 2, 0, 3)).reshape(up_weight.shape).astype(F32)
    down_grad = jnp.transpose(rd, (1, 0, 3, 2)).reshape(down_weight.shape).astype(F32)

    gain_grad = jnp.sum(gsum[:, 12, : 4 * head_dim], axis=0).reshape(norm_gain.shape)
    mod_rows = gsum[:, :12].reshape(n_seq, 2, 1, 6, dim)
    cond_col = cond_act.astype(F32)[:, None, :, None, None]
    mod_grad = jnp.sum(cond_col * mod_rows, axis=0)[None]

    results = [img_out, txt_out, img_grad, txt_grad]
    for weight, moment, second, grad in (
        (mod_weight, mod_moment, mod_second, mod_grad),
        (qkv_weight, qkv_moment, qkv_second, qkv_grad),
        (out_weight, out_moment, out_second, out_grad),
        (up_weight, up_moment, up_second, up_grad),
        (down_weight, down_moment, down_second, down_grad),
        (norm_gain, gain_moment, gain_second, gain_grad),
    ):
        results.append(grad)
        results.extend(adam_step(weight, moment, second, grad))
    return tuple(results)


def fits_split(mesh, args):
    dp, zn, tp = (mesh.shape[axis] for axis in ALL)
    img, txt, gain, qkv, up = args[0], args[1], args[8], args[4], args[6]
    heads = qkv.shape[4] // gain.shape[-1]
    return (
        dp == 4
        and tp == 2
        and zn > 1
        and qkv.shape[0] == 1
        and img.shape[0] == dp
        and heads % (tp * zn) == 0
        and (4 * qkv.shape[4] // (tp * zn)) % 128 == 0
        and (up.shape[3] // (tp * zn)) % 128 == 0
        and img.shape[1] % (zn * 2 * CHUNK) == 0
        and img.shape[2] % 128 == 0
        and img.shape[2] % (dp * zn * CHUNK) == 0
        and 4 * gain.shape[-1] <= img.shape[2]
    )


def solution(mesh):
    tokens = [P(DP, CTX, None), P(DP, None, None)]
    mod_spec = P(None, None, ALL, None, None)
    qkv_spec = P(None, None, ROWS, None, TP)
    out_spec = P(None, None, TP, ROWS)
    up_spec = P(None, None, ROWS, TP)
    weights = [mod_spec, qkv_spec, out_spec, up_spec, out_spec, P()]
    in_specs = tuple(tokens + [P(None, ALL)] + weights + tokens + weights + weights)
    out_specs = tuple(tokens + tokens + [spec for spec in weights for _ in range(4)])

    def step(*args):
        body = split_body if fits_split(mesh, args) else gathered_body
        return jax.shard_map(
            body, mesh=mesh, in_specs=in_specs, out_specs=out_specs, check_vma=False
        )(*args)

    return step
```

profile of v0, /device:TPU:0, one launch (start us, length us, event | category | flops | bytes accessed | tf_op | source)
XLA Modules:
  0.0 728.2 jit_solution(2801224477554096596)
XLA Ops:
  7.0 2.6 pad_maximum_fusion.5.wa
  15.0 3.6 convert_element_type.326
  22.3 3.0 dot_general.114
  27.9 177.9 %shard_map.438 = (bf16[2,16,96,768]{3,2,1,0:T(8,128)(2,1)}, bf16[2,16,96,768]{3,2,1,0:T(8,128)(2,1)}, bf16[2,16,96,768]{3,2,1,0:T(8,128)(2,1)}, bf16[4,2,64,1536...) custom-call(bf16[4,2,96,768]{3,2,1,0:T(8,128)(2,1)} %pad_maximum_fusion.5.wa, ...), custom_call_target="tpu_custom_call" | custom-call | tf_op jit(solution)/shard_map/pallas_call | solution.py:583
  205.7 3.7 slice_bitcast_fusion.1
  209.5 3.9 copy.125
  223.9 3.1 fusion.85
  233.7 2.9 fusion.81
  240.1 3.3 convolution_convert_fusion.9
  243.4 2.7 convolution_convert_fusion.13
  250.9 77.2 %shard_map.439 = (bf16[4,2,64,1536]{3,2,1,0:T(8,128)(2,1)}, bf16[4,2,32,1536]{3,2,1,0:T(8,128)(2,1)}, f32[96,1536]{1,0:T(8,128)}, f32[96,1536]{1,0:T(8,128)}) custom-call(bf16[4,2,64,1536]{3,2,1,0:T(8,128)(2,1)} %bitcast.322, bf16[4,2,32,1536]{3,2,1,0:T(8,128)(2,1)} %bitcast.337, bf16[96,1536]{1,0:T(8,128)(2,1)} %pad_maximum_fusion.7.xr_rows.x_rows, ...), custom_call_target="tpu_custom_call" | custom-call | tf_op jit(solution)/shard_map/pallas_call | solution.py:583
  328.1 4.0 fusion.31
  332.2 2.6 convolution_convert_fusion.8
  339.5 2.6 convolution_convert_fusion.7
  344.6 94.8 %shard_map.440 = (bf16[4,2,64,1536]{3,2,1,0:T(8,128)(2,1)}, bf16[4,2,32,1536]{3,2,1,0:T(8,128)(2,1)}, bf16[96,1536]{1,0:T(8,128)(2,1)}, f32[96,1536]{1,0:T(8,128)}, f32[2,4,1536]{2,1,0:T(4,128)}) custom-call(bf16[4,2,64,1536]{3,2,1,0:T(8,128)(2,1)} %bitcast.363, bf16[4,2,32,1536]{3,2,1,0:T(8,128)(2,1)} %bitcast.372, bf16[4,2,64,1536]{3,2,1,0:T(8,128)(2,1)} %bitcast.364, ...), custom_call_target="tpu_custom_call" | custom-call | tf_op jit(solution)/shard_map/pallas_call | solution.py:583
  439.4 3.2 slice_bitcast_fusion.3
  451.9 3.2 convolution_bitcast_fusion.1
  455.4 3.0 multiply_convert_fusion
  461.9 2.6 convolution_convert_fusion.6
  467.4 76.7 %shard_map.441 = (bf16[2,2,64,1536]{3,2,1,0:T(8,128)(2,1)}, bf16[2,4,2,32,1536]{4,3,2,1,0:T(8,128)(2,1)}, f32[4,16,1536]{2,1,0:T(8,128)}) custom-call(bf16[4,2,64,1536]{3,2,1,0:T(8,128)(2,1)} %bitcast.362, bf16[4,2,32,1536]{3,2,1,0:T(8,128)(2,1)} %bitcast.374, bf16[96,1536]{1,0:T(8,128)(2,1)} %pad_maximum_fusion.7.xr_rows.x_rows, ...), custom_call_target="tpu_custom_call" | custom-call | tf_op jit(solution)/shard_map/pallas_call | solution.py:583
  551.8 5.0 multiply_subtract_fusion
  563.8 2.6 copy.135
  566.5 5.1 pad_maximum_fusion.da
  574.6 2.6 pad_maximum_fusion.1.du
  581.3 2.6 pad_maximum_fusion.2.dd
  583.9 97.2 %shard_map.442 = (bf16[4,2,96,768]{3,2,1,0:T(8,128)(2,1)}, bf16[4,2,96,768]{3,2,1,0:T(8,128)(2,1)}, bf16[4,2,96,768]{3,2,1,0:T(8,128)(2,1)}) custom-call(bf16[2,16,96,768]{3,2,1,0:T(8,128)(2,1)} %pad_maximum_fusion.da, bf16[2,16,96,768]{3,2,1,0:T(8,128)(2,1)} %pad_maximum_fusion.1.du, bf16[2,16,96,768]{3,2,1,0:T(8,128)(2,1)} %pad_maximum_fusion.2.dd), custom_call_target="tpu_custom_call" | custom-call | tf_op jit(solution)/shard_map/pallas_call | solution.py:583
  681.1 2.6 slice_convert_fusion
  685.7 2.5 copy.138
  688.3 3.2 reshape.585
  691.4 5.9 multiply_subtract_fusion.3
  705.8 8.3 %multiply_subtract_fusion.2 = (f32[1,2,96,3072]{3,2,1,0:T(8,128)}, f32[1,2,96,3072]{3,2,1,0:T(8,128)}, f32[1,2,96,3072]{3,2,1,0:T(8,128)}) fusion(f32[1,2,96,3072]{3,2,1,0:T(8,128)} %param.29, f32[1,2,96,3072]{3,2,1,0:T(8,128)} %reshape.587, f32[1,2,96,3072]{3,2,1,0:T(8,128)} %param.37, f32[1,2,96,3072]{3,2,1,0:T(8,128)} %param.43), kind=kLoop, calls=%fused_computation.52 | loop fusion | flops 8847360 | bytes 16515072 | tf_op jit(solution)/shard_map/sub | solution.py:65
  718.1 8.2 %multiply_subtract_fusion.1 = (f32[1,2,3072,96]{2,3,1,0:T(8,128)}, f32[1,2,3072,96]{2,3,1,0:T(8,128)}, f32[1,2,3072,96]{2,3,1,0:T(8,128)}) fusion(f32[1,2,3072,96]{2,3,1,0:T(8,128)} %param.30, f32[1,2,3072,96]{2,3,1,0:T(8,128)} %reshape.588, f32[1,2,3072,96]{2,3,1,0:T(8,128)} %param.38, f32[1,2,3072,96]{2,3,1,0:T(8,128)} %param.44), kind=kLoop, calls=%fused_computation.50 | loop fusion | flops 8847360 | bytes 16515072 | tf_op jit(solution)/shard_map/sub | solution.py:65
  (347 shorter events, 103.1 us)
Async XLA Ops:
  15.0 6.0 copy-start.3
  217.0 22.2 %copy-start.15 = (f32[256,3,3,64]{0,3,2,1:T(8,128)}, f32[256,3,3,64]{0,3,2,1:T(8,128)S(1)}, u32[]{:S(2)}) copy-start(f32[256,3,3,64]{0,3,2,1:T(8,128)S(1)} %fusion.39) | copy-start | bytes 1769476
  217.0 10.1 %copy-start.80 = (f32[64]{0:T(128)}, f32[64]{0:T(128)S(1)}, u32[]{:S(2)}) copy-start(f32[64]{0:T(128)S(1)} %get-tuple-element.130) | copy-start | bytes 772
  217.1 10.1 %copy-start.82 = (f32[64]{0:T(128)}, f32[64]{0:T(128)S(1)}, u32[]{:S(2)}) copy-start(f32[64]{0:T(128)S(1)} %get-tuple-element.133) | copy-start | bytes 772
  217.3 10.1 %copy-start.40 = (bf16[256,3,64]{0,2,1:T(8,128)(2,1)}, bf16[256,3,64]{0,2,1:T(8,128)(2,1)S(1)}, u32[]{:S(2)}) copy-start(bf16[256,3,64]{0,2,1:T(8,128)(2,1)S(1)} %get-tuple-element.123) | copy-start | bytes 294916
  217.3 10.1 %copy-start.42 = (bf16[256,3,64]{0,2,1:T(8,128)(2,1)}, bf16[256,3,64]{0,2,1:T(8,128)(2,1)S(1)}, u32[]{:S(2)}) copy-start(bf16[256,3,64]{0,2,1:T(8,128)(2,1)S(1)} %get-tuple-element.122) | copy-start | bytes 294916
  227.0 12.2 %copy-start.6 = (f32[512,3,3,64]{0,3,2,1:T(8,128)}, f32[512,3,3,64]{0,3,2,1:T(8,128)S(1)}, u32[]{:S(2)}) copy-start(f32[512,3,3,64]{0,3,2,1:T(8,128)S(1)} %fusion.85) | copy-start | bytes 3538948
  227.4 6.1 slice-start.6
  233.5 5.8 copy-start.1
  240.0 6.1 copy-start.18
  240.1 6.1 copy-start.55
  240.1 6.0 copy-start.30
  240.1 6.7 copy-start.46
  246.8 81.2 %copy-start.27 = (bf16[1,16,96,768]{3,2,1,0:T(8,128)(2,1)S(1)}, bf16[1,16,96,768]{3,2,1,0:T(8,128)(2,1)}, u32[]{:S(2)}) copy-start(bf16[1,16,96,768]{3,2,1,0:T(8,128)(2,1)} %get-tuple-element.140) | copy-start | bytes 7077892
  332.1 7.2 copy-start.103
  336.2 5.9 copy-start.101
  442.6 12.7 %slice-start = ((s8[7077888]{0:T(1024)(128)(4,1)}), s8[2883584]{0:T(1024)(128)(4,1)S(1)}, s32[]{:S(2)}) async-start(s8[7077888]{0:T(1024)(128)(4,1)} %bitcast.307), calls=%async_computation | async-start | bytes 5767168
  449.5 5.8 slice-start.1
  544.1 7.0 copy-start.21
  551.0 5.8 copy-start.2
  551.8 5.3 copy-start.19
  551.8 5.4 copy-start.86
  551.8 5.4 copy-start.88
  551.8 5.4 copy-start.95
  551.8 5.4 copy-start.99
  566.5 5.1 copy-start.51
  566.5 5.1 copy-start.60
  691.4 5.9 copy-start.12
  705.8 8.3 %copy-start.38 = (bf16[4,2,96,768]{3,2,1,0:T(8,128)(2,1)S(1)}, bf16[4,2,96,768]{3,2,1,0:T(8,128)(2,1)}, u32[]{:S(2)}) copy-start(bf16[4,2,96,768]{3,2,1,0:T(8,128)(2,1)} %get-tuple-element.69) | copy-start | bytes 3538948
  718.1 9.1 %copy-start.90 = (f32[1,2,2,64]{3,2,1,0:T(2,128)S(1)}, f32[1,2,2,64]{3,2,1,0:T(2,128)}, u32[]{:S(2)}) copy-start(f32[1,2,2,64]{3,2,1,0:T(2,128)} %param.31) | copy-start | bytes 3076
  718.1 9.1 %copy-start.96 = (f32[1,2,2,64]{3,2,1,0:T(2,128)S(1)}, f32[1,2,2,64]{3,2,1,0:T(2,128)}, u32[]{:S(2)}) copy-start(f32[1,2,2,64]{3,2,1,0:T(2,128)} %param.39) | copy-start | bytes 3076
  718.1 9.1 %copy-start.97 = (f32[1,2,2,64]{3,2,1,0:T(2,128)S(1)}, f32[1,2,2,64]{3,2,1,0:T(2,128)}, u32[]{:S(2)}) copy-start(f32[1,2,2,64]{3,2,1,0:T(2,128)} %param.45) | copy-start | bytes 3076
  (83 other events, 207.0 us)
where the time goes:
time: 740 us; the launch traced here: 728 us
  Pallas kernels  524 us (71%)
  local copies, waits for them, and re-layouts  77.7 us (10%)
  other arithmetic  65.6 us (9%)
  matrix products  58.4 us (8%)
    pallas_call x5, Pallas kernels, call(): pl.pallas_call(kernel, out_shape=[shape for shape, _ in outs], in_specs=i...  524 us
    dot_general x24, matrix products, dot(): lax.dot_general(one, two, ((dims[:1], dims[1:]), ((), ())), preferred_ele...  46.3 us
    sub x6, other arithmetic, adam_step(): return (weight - learn_rate * update, new_moment, new_second)  29.4 us
    dot_general x6, local copies, waits for them, and re-layouts, dot(): lax.dot_general(one, two, ((dims[:1], dims[1:]), ((), ())), preferred_ele...  17.7 us

commit v1 on v0

--- a/solution.py
+++ b/solution.py
@@ -596,142 +596,7 @@
     return jax.ShapeDtypeStruct(shape, dtype)
 
 
-def spread_kernel(
-    zn, wa, wu, wd, xi, ci, mp, ga, gu, gd, xo, co, mod,
-    bw, bx, my, m2, mc, m1, mx, slots,
-    zs, zr, ys, yr, cs, cr, xs, xr, ms, mr, loc,
-):
-    me = Place(zn)
-    me.greet()
-    d, c, t, y, k = me.d, me.c, me.t, me.y, me.k
-    outs = (ga, gu, gd)
-    own = []
-    bounce = []
-    for kind, w in enumerate((wa, wu, wd)):
-        bounce.append(local(w.at[c], bw.at[kind], loc.at[kind]))
-    for act, a in enumerate((xi, ci)):
-        bounce.append(local(a, bx.at[act], loc.at[3 + act]))
-    pending = []
-    m_y = remote(mp.at[pl.ds((1 - y) * 2, 2)], my, ms.at[0], mr.at[0], {DP: me.d_y})
-    zcopies = {}
-
-    def send_tokens(act, a, o):
-        zcopies[6 + act] = [
-            remote(a.at[t], o.at[c, t], zs.at[6 + act, s - 1], zr.at[6 + act, s - 1], {CTX: me.ahead(s)})
-            for s in range(1, zn)
-        ]
-
-    def send_weights(kind, w):
-        for st in range(2):
-            zcopies[kind * 2 + st] = [
-                remote(
-                    w.at[me.ahead(s), st],
-                    outs[kind].at[st, d * zn + c],
-                    zs.at[kind * 2 + st, s - 1],
-                    zr.at[kind * 2 + st, s - 1],
-                    {CTX: me.ahead(s)},
-                )
-                for s in range(1, zn)
-            ]
-
-    send_tokens(0, xi, xo)
-    send_weights(0, wa)
-    send_weights(1, wu)
-    send_weights(2, wd)
-    send_tokens(1, ci, co)
-
-    for kind in range(3):
-        bounce[kind].wait()
-        for st in range(2):
-            own.append(local(bw.at[kind, st], outs[kind].at[st, d * zn + c], loc.at[5 + kind * 2 + st]))
-    for act, o in enumerate((xo, co)):
-        bounce[3 + act].wait()
-        own.append(local(bx.at[act], o.at[c], loc.at[11 + act]))
-
-    m_y.wait()
-    m2[...] = mp[pl.ds(y * 2, 2)] + my[...]
-    m_c = remote(m2.at[1 - k], mc, ms.at[1], mr.at[1], {DP: me.d_core})
-    m_c.wait()
-    m1[...] = m2[k] + mc[...]
-    m_x = remote(m1, mx, ms.at[2], mr.at[2], {TP: me.t_x})
-    m_x.wait()
-    slots[c] = m1[...] + mx[...]
-    m_z = [
-        remote(slots.at[c], slots.at[c], ms.at[2 + s], mr.at[2 + s], {CTX: me.ahead(s)})
-        for s in range(1, zn)
-    ]
-
-    def forward_tokens(act, o):
-        for s in range(1, zn):
-            zcopies[6 + act][s - 1].wait()
-            src = me.behind(s)
-            pending.append(
-                remote(o.at[src, t], o.at[src, t], xs.at[act, s - 1], xr.at[act, s - 1], {TP: me.t_x})
-            )
-
-    forward_tokens(0, xo)
-    ycopies = []
-    for chunk in range(6):
-        kind, st = divmod(chunk, 2)
-        g = outs[kind]
-        for copy in zcopies[chunk]:
-            copy.wait()
-        own[chunk].wait()
-        mine = g.at[st, pl.ds(d * zn, zn)]
-        ycopies.append(remote(mine, mine, ys.at[chunk], yr.at[chunk], {DP: me.d_y}))
-        pending.append(remote(mine, mine, cs.at[chunk, 0], cr.at[chunk, 0], {DP: me.d_core}))
-        if chunk:
-            pass_on(me, outs, chunk - 1, ycopies, pending, cs, cr)
-        if chunk == 1:
-            for copy in m_z:
-                copy.wait()
-            total = slots[0]
-            for z in range(1, zn):
-                total = total + slots[z]
-            mod[...] = total
-    forward_tokens(1, co)
-    pass_on(me, outs, 5, ycopies, pending, cs, cr)
-    for copy in pending:
-        copy.wait()
-    for copy in own[6:]:
-        copy.wait()
-
-
-def pass_on(me, outs, chunk, ycopies, pending, cs, cr):
-    kind, st = divmod(chunk, 2)
-    ycopies[chunk].wait()
-    there = outs[kind].at[st, pl.ds(me.d_y * me.zn, me.zn)]
-    pending.append(remote(there, there, cs.at[chunk, 1], cr.at[chunk, 1], {DP: me.d_core}))
-
-
-def spread(zn, wa, wu, wd, xi, ci, mp):
-    rows, width = wa.shape[2:]
-    half, dim = xi.shape[1:]
-    lines = mp.shape[1]
-    weight = shaped((2, 4 * zn, rows, width), BF)
-    token = shaped((zn, 2, half, dim), BF)
-    return call(
-        functools.partial(spread_kernel, zn),
-        0,
-        [HBM] * 5 + [VMEM],
-        [(weight, HBM)] * 3 + [(token, HBM)] * 2 + [(shaped((lines, 128), F32), VMEM)],
-        [
-            pltpu.VMEM((3, 2, rows, width), BF),
-            pltpu.VMEM((2, 2, half, dim), BF),
-            pltpu.VMEM((2, lines, 128), F32),
-            pltpu.VMEM((2, lines, 128), F32),
-            pltpu.VMEM((lines, 128), F32),
-            pltpu.VMEM((lines, 128), F32),
-            pltpu.VMEM((lines, 128), F32),
-            pltpu.VMEM((zn, lines, 128), F32),
-            DMA((8, zn)), DMA((8, zn)), DMA((6,)), DMA((6,)), DMA((6, 2)), DMA((6, 2)),
-            DMA((2, zn)), DMA((2, zn)), DMA((2 + zn,)), DMA((2 + zn,)), DMA((13,)),
-        ],
-        (wa, wu, wd, xi, ci, mp),
-    )
-
-
-CHUNK = 16
+CHUNK = 8
 
 
 def sum_start(me, arrays, own, recvx, xs, xr, loc):
@@ -865,65 +730,276 @@
     ]
 
 
-def middle_kernel(
-    zn, sizes, pi, pt, xr_rows, mod, hi, ht, resid, proj,
-    own, recvx, sumb, recvz, total, sxs, sxr, sloc, szs, szr,
-    hb, gzs, gzr, gxs, gxr, gloc,
-):
+class PairSum:
+    def __init__(self, me, grads, outs, crecv, part, yrecv, cs, cr, ys, yr, ls):
+        self.me, self.grads, self.outs = me, grads, outs
+        self.crecv, self.part, self.yrecv = crecv, part, yrecv
+        self.cs, self.cr, self.ys, self.yr, self.ls = cs, cr, ys, yr, ls
+        self.chunks = [(kind, st) for kind in range(grads.shape[0]) for st in range(2)]
+        self.first, self.second, self.last = {}, {}, []
+        self.span = yrecv.shape[1]
+
+    def rows(self, y, core, more=0, n=None):
+        first = (y * 2 + core) * self.span + more
+        return pl.ds(pl.multiple_of(first, 16), n or self.span)
+
+    def start(self, at):
+        me = self.me
+        kind, st = self.chunks[at]
+        for j, yy in enumerate((1 - me.y, me.y)):
+            self.first[at, j] = remote(
+                self.grads.at[kind, st, self.rows(yy, 1 - me.k)],
+                self.crecv.at[at, j],
+                self.cs.at[at, j],
+                self.cr.at[at, j],
+                {DP: me.d_core},
+            )
+
+    def across(self, at):
+        me = self.me
+        kind, st = self.chunks[at]
+        for j, yy in enumerate((1 - me.y, me.y)):
+            self.first[at, j].wait()
+
+            @pl.loop(0, self.span // 16)
+            def _(i, j=j, yy=yy):
+                to = pl.ds(pl.multiple_of(i * 16, 16), 16)
+                mine = self.grads[kind, st, self.rows(yy, me.k, i * 16, 16)]
+                self.part[at, j, to] = (mine.astype(F32) + self.crecv[at, j, to].astype(F32)).astype(BF)
+
+            if j == 0:
+                self.second[at] = remote(
+                    self.part.at[at, 0], self.yrecv.at[at], self.ys.at[at], self.yr.at[at], {DP: me.d_y}
+                )
+
+    def end(self):
+        me = self.me
+        each = self.span // me.zn
+        for at, (kind, st) in enumerate(self.chunks):
+            self.second[at].wait()
+
+            @pl.loop(0, self.span // 16)
+            def _(i, at=at):
+                to = pl.ds(pl.multiple_of(i * 16, 16), 16)
+                self.crecv[at, 0, to] = (
+                    self.part[at, 1, to].astype(F32) + self.yrecv[at, to].astype(F32)
+                ).astype(BF)
+
+            for s in range(me.zn):
+                rows = pl.ds(pl.multiple_of(me.ahead(s) * each, 16), each)
+                self.last.append(
+                    local(self.crecv.at[at, 0, rows], self.outs[s].at[kind, st], self.ls.at[at, s])
+                )
+        for copy in self.last:
+            copy.wait()
+
+
+def pair_scratch(kinds, zn, rows, width):
+    n = 2 * kinds
+    return [
+        pltpu.VMEM((n, 2, zn * rows, width), BF),
+        pltpu.VMEM((n, 2, zn * rows, width), BF),
+        pltpu.VMEM((n, zn * rows, width), BF),
+        DMA((n, 2)), DMA((n, 2)), DMA((n,)), DMA((n,)), DMA((n, zn)),
+    ]
+
+
+def pair_outs(kinds, zn, rows, width):
+    return [(shaped((kinds, 2, rows, width), BF), HBM)] * zn
+
+
+GELU_ONE = 0.7978845608028654
+GELU_TWO = 0.044715
+
+
+def gelu_both(p):
+    square = p * p
+    th = jnp.tanh(GELU_ONE * (p + GELU_TWO * p * square))
+    half = 0.5 * (1.0 + th)
+    slope = half + 0.5 * p * (1.0 - th * th) * GELU_ONE * (1.0 + 3.0 * GELU_TWO * square)
+    return p * half, slope
+
+
+class RowSum:
+    def __init__(self, me, sizes, img, txt, recvx, sumb, recvz, total, xs, xr, zs, zr):
+        self.me, self.sizes, self.img, self.txt = me, sizes, img, txt
+        self.recvx, self.sumb, self.recvz, self.total = recvx, sumb, recvz, total
+        self.xs, self.xr, self.zs, self.zr = xs, xr, zs, zr
+        self.sent, self.over_z = {}, []
+
+    def send(self, s):
+        me, (n_img, n_txt) = self.me, self.sizes
+        zb = me.ahead(s)
+        theirs = pl.ds(pl.multiple_of((zb * 2 + me.t_x) * n_img, n_img), n_img)
+        where = {TP: me.t_x}
+        self.sent[s] = [
+            remote(
+                self.img.at[theirs], self.recvx.at[s, pl.ds(0, n_img)], self.xs.at[s, 0], self.xr.at[s, 0], where
+            ),
+            remote(
+                self.txt.at[zb, me.t_x],
+                self.recvx.at[s, pl.ds(n_img, n_txt)],
+                self.xs.at[s, 1],
+                self.xr.at[s, 1],
+                where,
+            ),
+        ]
+
+    def add(self, s):
+        me, (n_img, n_txt) = self.me, self.sizes
+        zb = me.ahead(s)
+        for copy in self.sent[s]:
+            copy.wait()
+
+        def put(to, value):
+            if s:
+                self.sumb[s, to] = value.astype(BF)
+            else:
+                self.total[to] = value
+
+        @pl.loop(0, n_img // STEP)
+        def _(i):
+            to = pl.ds(pl.multiple_of(i * STEP, STEP), STEP)
+            at = pl.ds(pl.multiple_of((zb * 2 + me.t) * n_img + i * STEP, STEP), STEP)
+            put(to, self.img[at].astype(F32) + self.recvx[s, to].astype(F32))
+
+        to = pl.ds(n_img, n_txt)
+        put(to, self.txt[zb, me.t].astype(F32) + self.recvx[s, to].astype(F32))
+        if s:
+            self.over_z.append(
+                remote(self.sumb.at[s], self.recvz.at[s], self.zs.at[s], self.zr.at[s], {CTX: zb})
+            )
+
+    def arrive(self):
+        for copy in self.over_z:
+            copy.wait()
+
+    def rows(self, at):
+        value = self.total[at]
+        for s in range(1, self.me.zn):
+            value = value + self.recvz[s, at].astype(F32)
+        return value
+
+
+def row_scratch(zn, sizes, dim):
+    n_img, n_txt = sizes
+    block = n_img + n_txt
+    return [
+        pltpu.VMEM((2 * zn * n_img, dim), BF),
+        pltpu.VMEM((zn, 2, n_txt, dim), BF),
+        pltpu.VMEM((zn, block, dim), BF),
+        pltpu.VMEM((zn, block, dim), BF),
+        pltpu.VMEM((zn, block, dim), BF),
+        pltpu.VMEM((block, dim), F32),
+        DMA((zn, 2)), DMA((zn, 2)), DMA((zn,)), DMA((zn,)),
+    ]
+
+
+ROW_SCRATCH = 10
+
+
+def turn_kernel(zn, sizes, *refs):
+    take = iter(refs)
+    him, htx, cim, ctx, resid, proj, mod, gu, gd, ctx4 = [next(take) for _ in range(10)]
+    bi, bt, out, rgrad, sums = [next(take) for _ in range(5)]
+    pieces = [next(take) for _ in range(zn)]
+    up, down, act, pre, branch, grads, cotr = [next(take) for _ in range(7)]
+    h_refs = [next(take) for _ in range(ROW_SCRATCH)]
+    m_refs = [next(take) for _ in range(ROW_SCRATCH)]
+    bb, gzs, gzr, gxs, gxr, gloc = [next(take) for _ in range(6)]
+    pair_refs = [next(take) for _ in range(8)]
+    (loc,) = take
     me = Place(zn)
-    me.greet(core=False, y=False)
-    copies = sum_start(me, [(pi, pt)], own, recvx, sxs, sxr, sloc)
-    zc = sum_x(me, 0, copies, own, recvx, sumb, recvz, total, szs, szr)
-    sum_z(me, 0, zc, recvz, total)
+    n_img, n_txt = sizes
+    img_all = 2 * zn * n_img
+    h_sum, m_sum = RowSum(me, sizes, *h_refs), RowSum(me, sizes, *m_refs)
+    pair = PairSum(me, grads, pieces, *pair_refs)
+    load_up = local(gu, up, loc.at[0])
+    load_down = local(gd, down, loc.at[1])
+    mine = pl.ds(pl.multiple_of((me.c * 2 + me.t) * n_img, n_img), n_img)
+    load_cot = [
+        local(cim.at[mine], cotr.at[pl.ds(0, n_img)], loc.at[2]),
+        local(ctx4.at[me.c, me.t], cotr.at[pl.ds(n_img, n_txt)], loc.at[3]),
+    ]
+    me.greet()
+    load_up.wait()
+    load_down.wait()
+
+    def text_rows(ref, value):
+        for zb in range(zn):
+            for half in range(2):
+                first = (zb * 2 + half) * n_txt
+                ref[zb, half] = value[first : first + n_txt].astype(BF)
+
+    def front_half(stream, hidden, cot, places):
+        p = dot(hidden, up[stream], (1, 0))
+        activated, slope = gelu_both(p)
+        low = (cot.astype(F32) * line(mod, stream, 5)).astype(BF)
+        grad = (dot(low, down[stream], (1, 0)) * slope).astype(BF)
+        activated = activated.astype(BF)
+        at = 0
+        for place in places:
+            n = place.size
+            act[place] = activated[at : at + n]
+            pre[place] = grad[at : at + n]
+            branch[place] = low[at : at + n]
+            at += n
+        return dot(grad, up[stream], (1, 1))
+
+    txt_place = pl.ds(img_all, 2 * zn * n_txt)
+    text_rows(h_sum.txt, front_half(1, htx[...], ctx[...], [txt_place]))
+    order = list(range(1, zn)) + [0]
+    for first in range(0, zn, 2):
+        steps = order[first : first + 2]
+        places = [
+            pl.ds(pl.multiple_of(me.ahead(s) * 2 * n_img, 2 * n_img), 2 * n_img) for s in steps
+        ]
+        value = front_half(
+            0,
+            jnp.concatenate([him[place] for place in places], axis=0),
+            jnp.concatenate([cim[place] for place in places], axis=0),
+            places,
+        ).astype(BF)
+        for n, (s, place) in enumerate(zip(steps, places)):
+            h_sum.img[place] = value[n * 2 * n_img : (n + 1) * 2 * n_img]
+            h_sum.send(s)
+    text_rows(m_sum.txt, dot(act[txt_place], down[1], (1, 1)))
+    for first in range(0, img_all, 256):
+        rows = slice(first, first + 256)
+        m_sum.img[rows] = dot(act[rows], down[0], (1, 1)).astype(BF)
+    for s in order:
+        m_sum.send(s)
+    h_sum.add(order[0])
+    parts = ((0, pl.ds(0, img_all)), (1, txt_place))
+    dim = him.shape[1]
+
+    def gradient(kind, at):
+        stream, place = parts[at % 2]
+        for first in range(0, dim, 256):
+            d = slice(first, first + 256)
+            if kind == 0:
+                left = him[:, d] if stream == 0 else htx[:, d]
+                value = dot(left, pre[place], (0, 0))
+            else:
+                value = dot(branch[place, d], act[place], (0, 0))
+            grads[kind, stream, d] = value.astype(BF)
+        pair.start(kind * 2 + stream)
+
+    work = [lambda n=n: gradient(*divmod(n, 2)) for n in range(4)]
+    for n, s in enumerate(order[1:]):
+        work[n]()
+        h_sum.add(s)
+    work[3]()
+    sums[...] = jnp.zeros_like(sums)
+    pair.across(0)
+    h_sum.arrive()
+    for copy in load_cot:
+        copy.wait()
 
     def rows(stream, at):
-        p = total[0, at]
-        proj[at] = p
-        value = xr_rows[at].astype(F32) + line(mod, stream, 2) * p
-        resid[at] = value
-        normed, _ = layer_norm(value)
-        hb[at] = (normed * (1.0 + line(mod, stream, 4)) + line(mod, stream, 3)).astype(BF)
-
-    row_loops(sizes, rows)
-    copies = share_start(me, hb, (hi, ht), sizes, gzs, gzr, gxs, gxr, gloc)
-    share_end(me, copies, (hi, ht), gxs, gxr)
-
-
-def middle(zn, sizes, pi, pt, rows, mod):
-    dim = rows.shape[1]
-    total = sum(sizes)
-    return call(
-        functools.partial(middle_kernel, zn, sizes),
-        1,
-        [HBM, HBM, VMEM, VMEM],
-        [
-            (shaped(pi.shape, BF), HBM),
-            (shaped(pt.shape, BF), HBM),
-            (shaped((total, dim), F32), VMEM),
-            (shaped((total, dim), F32), VMEM),
-        ],
-        sum_scratch(1, zn, total, dim) + share_scratch(zn, total, dim),
-        (pi, pt, rows, mod),
-    )
-
-
-def turn_kernel(
-    zn, sizes, hi, ht, mi, mt, resid, proj, cot, mod, bi, bt, out, rgrad, sums,
-    own, recvx, sumb, recvz, total, sxs, sxr, sloc, szs, szr,
-    bb, gzs, gzr, gxs, gxr, gloc,
-):
-    me = Place(zn)
-    me.greet(core=False, y=False)
-    copies = sum_start(me, [(hi, ht), (mi, mt)], own, recvx, sxs, sxr, sloc)
-    zh = sum_x(me, 0, copies, own, recvx, sumb, recvz, total, szs, szr)
-    sums[...] = jnp.zeros_like(sums)
-    sum_z(me, 0, zh, recvz, total)
-
-    def rows(stream, at):
-        h = total[0, at]
+        h = h_sum.rows(at)
         normed, spread_ = layer_norm(resid[at])
-        g = cot[at].astype(F32)
-        value = g + norm_back(h * (1.0 + line(mod, stream, 4)), normed, spread_)
+        value = cotr[at].astype(F32) + norm_back(h * (1.0 + line(mod, stream, 4)), normed, spread_)
         rgrad[at] = value
         bb[at] = (value * line(mod, stream, 2)).astype(BF)
         sums[stream, 0] += jnp.sum(value * proj[at], axis=0)
@@ -932,46 +1008,75 @@
 
     row_loops(sizes, rows)
     shared = share_start(me, bb, (bi, bt), sizes, gzs, gzr, gxs, gxr, gloc)
-    zm = sum_x(me, 1, copies, own, recvx, sumb, recvz, total, szs, szr)
+    for s in order:
+        m_sum.add(s)
+    for n in range(1, 4):
+        pair.across(n)
     share_end(me, shared, (bi, bt), gxs, gxr)
-    sum_z(me, 1, zm, recvz, total)
-
-    def tail(stream, at):
-        m = total[1, at]
+    m_sum.arrive()
+
+    def last(stream, at):
+        m = m_sum.rows(at)
         out[at] = (resid[at] + line(mod, stream, 5) * m).astype(BF)
-        sums[stream, 3] += jnp.sum(cot[at].astype(F32) * m, axis=0)
-
-    row_loops(sizes, tail)
-
-
-def turn(zn, sizes, hi, ht, mi, mt, resid, proj, cot, mod):
+        sums[stream, 3] += jnp.sum(cotr[at].astype(F32) * m, axis=0)
+
+    row_loops(sizes, last)
+    pair.end()
+
+
+def turn(zn, sizes, him, htx, cim, ctx, resid, proj, mod, gu, gd):
     total, dim = resid.shape
+    n_img, n_txt = sizes
+    ff = gu.shape[2]
+    rows = dim // (4 * zn)
+    every = 2 * zn * total
+    ctx4 = ctx.reshape(zn, 2, n_txt, dim)
     return call(
         functools.partial(turn_kernel, zn, sizes),
         2,
-        [HBM] * 4 + [VMEM] * 4,
+        [VMEM] * 7 + [HBM] * 3,
         [
-            (shaped(hi.shape, BF), HBM),
-            (shaped(ht.shape, BF), HBM),
+            (shaped((zn, 2, n_img, dim), BF), HBM),
+            (shaped((zn, 2, n_txt, dim), BF), HBM),
             (shaped((total, dim), BF), VMEM),
             (shaped((total, dim), F32), VMEM),
             (shaped((2, 4, dim), F32), VMEM),
-        ],
-        sum_scratch(2, zn, total, dim) + share_scratch(zn, total, dim),
-        (hi, ht, mi, mt, resid, proj, cot, mod),
+        ]
+        + pair_outs(2, zn, rows, ff),
+        [
+            pltpu.VMEM((2, dim, ff), BF),
+            pltpu.VMEM((2, dim, ff), BF),
+            pltpu.VMEM((every, ff), BF),
+            pltpu.VMEM((every, ff), BF),
+            pltpu.VMEM((every, dim), BF),
+            pltpu.VMEM((2, 2, dim, ff), BF),
+            pltpu.VMEM((total, dim), BF),
+        ]
+        + row_scratch(zn, sizes, dim)
+        + row_scratch(zn, sizes, dim)
+        + share_scratch(zn, total, dim)
+        + pair_scratch(2, zn, rows, ff)
+        + [DMA((4,))],
+        (him, htx, cim, ctx, resid, proj, mod, gu, gd, ctx4),
     )
 
 
 def finish_kernel(
-    zn, sizes, ai, at_, x_rows, rgrad, out, sums, gains, mod, oi, ot, gsum,
-    own, recvx, sumb, recvz, total, sxs, sxr, sloc, szs, szr,
-    ob, msum, mx, slots, xs, xr, zs, zr, fs, fr, loc, ms, mr,
+    zn, sizes, ai, at_, x_rows, rgrad, out, sums, gains, mod, da, oi, ot, gsum, *rest
 ):
     me = Place(zn)
+    pieces, rest = rest[:zn], rest[zn:]
+    (
+        own, recvx, sumb, recvz, total, sxs, sxr, sloc, szs, szr,
+        ob, msum, mx, slots, xs, xr, zs, zr, fs, fr, loc, ms, mr,
+    ) = rest[:23]
+    pair = PairSum(me, da, pieces, *rest[23:])
     me.greet()
     c, t = me.c, me.t
     n_img, n_txt = sizes
     copies = sum_start(me, [(ai, at_)], own, recvx, sxs, sxr, sloc)
+    for n in range(2):
+        pair.start(n)
 
     def keep(stream, at):
         ob[0, at] = out[at]
@@ -979,6 +1084,8 @@
     row_loops(sizes, keep)
     zc = sum_x(me, 0, copies, own, recvx, sumb, recvz, total, szs, szr)
     msum[...] = jnp.zeros_like(msum)
+    for n in range(2):
+        pair.across(n)
     sum_z(me, 0, zc, recvz, total)
 
     def rows(stream, at):
@@ -1025,25 +1132,28 @@
     gsum[me.d] = value
     m_c = remote(gsum.at[me.d], gsum.at[me.d], ms.at[zn], mr.at[zn], {DP: me.d_core})
     m_c.wait()
-    pair = gsum.at[pl.ds(me.y * 2, 2)]
-    m_y = remote(pair, pair, ms.at[zn + 1], mr.at[zn + 1], {DP: me.d_y})
+    both = gsum.at[pl.ds(me.y * 2, 2)]
+    m_y = remote(both, both, ms.at[zn + 1], mr.at[zn + 1], {DP: me.d_y})
+    pair.end()
     m_y.wait()
     for copy in done:
         copy.wait()
 
 
-def finish(zn, sizes, ai, at_, x_rows, rgrad, out, sums, gains, mod):
+def finish(zn, sizes, ai, at_, x_rows, rgrad, out, sums, gains, mod, da):
     total, dim = rgrad.shape
+    rows, width = dim // (4 * zn), da.shape[3]
     n_img, n_txt = sizes
     return call(
         functools.partial(finish_kernel, zn, sizes),
         3,
-        [HBM] * 2 + [VMEM] * 6,
+        [HBM] * 2 + [VMEM] * 7,
         [
             (shaped((2, 2, n_img, dim), BF), HBM),
             (shaped((2, zn, 2, n_txt, dim), BF), HBM),
             (shaped((4, 16, dim), F32), VMEM),
-        ],
+        ]
+        + pair_outs(1, zn, rows, width),
         sum_scratch(1, zn, total, dim)
         + [
             pltpu.VMEM((2, total, dim), BF),
@@ -1052,98 +1162,672 @@
             pltpu.VMEM((zn, 16, dim), F32),
             DMA((2,)), DMA((2,)), DMA((zn,)), DMA((zn,)), DMA((zn,)), DMA((zn,)), DMA((2,)),
             DMA((zn + 2,)), DMA((zn + 2,)),
-        ],
-        (ai, at_, x_rows, rgrad, out, sums, gains, mod),
-    )
-
-
-def return_kernel(
-    zn, da, du, dd, ra, ru, rd, own, crecv, part, yrecv,
-    loc, cs, cr, ys, yr, zs, zr, ls,
-):
+        ]
+        + pair_scratch(1, zn, rows, width),
+        (ai, at_, x_rows, rgrad, out, sums, gains, mod, da),
+    )
+
+
+def over_ctx(zn, pieces):
+    return [pieces[0]] + [
+        lax.ppermute(pieces[s], CTX, [(i, (i + s) % zn) for i in range(zn)]) for s in range(1, zn)
+    ]
+
+
+def own_call(kernel, ins, outs, scratch, args, flops, moved):
+    return pl.pallas_call(
+        kernel,
+        out_shape=[shape for shape, _ in outs],
+        in_specs=ins,
+        out_specs=[spec for _, spec in outs],
+        scratch_shapes=scratch,
+        compiler_params=pltpu.CompilerParams(vmem_limit_bytes=60 * 1024 * 1024),
+        cost_estimate=pl.CostEstimate(flops=flops, bytes_accessed=moved, transcendentals=0),
+    )(*args)
+
+
+def dot(one, two, dims):
+    return lax.dot_general(one, two, ((dims[:1], dims[1:]), ((), ())), preferred_element_type=F32)
+
+
+STEP = 16
+EXP_MIN = -1e30
+
+
+def blocks_of(sizes, largest):
+    at = 0
+    for stream, n in enumerate(sizes):
+        size = largest if n % largest == 0 else n
+        for i in range(n // size):
+            yield stream, at + i * size, size
+        at += n
+
+
+def head_norms(packed, gains, stream, head, rows, heads):
+    wide = gains.shape[-1]
+    out = []
+    for which in range(2):
+        raw = packed[rows, (which * heads + head) * wide : (which * heads + head + 1) * wide]
+        normed, factor = rms_norm(raw)
+        out += [normed, factor]
+    value = packed[rows, (2 * heads + head) * wide : (2 * heads + head + 1) * wide]
+    return (*out, value)
+
+
+def fill_heads(packed, gains, sizes, heads, q_s, k_s, v_s):
+    for stream, first, size in blocks_of(sizes, 64):
+        rows = slice(first, first + size)
+        for head in range(heads):
+            q, _, k, _, v = head_norms(packed, gains, stream, head, rows, heads)
+            q_s[head, rows] = (q * gains[stream * 2][None, :]).astype(BF)
+            k_s[head, rows] = (k * gains[stream * 2 + 1][None, :]).astype(BF)
+            v_s[head, rows] = v.astype(BF)
+
+
+def forward_kernel(zn, live, sizes, heads, *refs):
+    take = iter(refs)
+    cond, modw, qkv, out, txt, gains = [next(take) for _ in range(6)]
+    up, down, xi, txt4, ci = [next(take) for _ in range(5)]
+    hidden_o, packed_o, lse_o, att_o, ga_o, hi, ht, co, gu, gd = [next(take) for _ in range(10)]
+    resid, proj, mod = [next(take) for _ in range(3)]
+    (
+        wa, mp, cbuf, pieces, ga, xo, xr, hidden, packed, lse, attended, q_s, k_s, v_s, flat, pim, ptx,
+        my, m2, mc, m1, mx, slots, recvx, sumb, recvz, total, hb, bx,
+        tzs, tzr, txs, txr, azs, azr, ays, ayr, acs, acr, ms, mr,
+        uzs, uzr, uys, uyr, ucs, ucr, sxs, sxr, szs, szr, gzs, gzr, gxs, gxr, gloc,
+        czs, czr, cxs, cxr, loc, uloc,
+    ) = take
     me = Place(zn)
+    d, c, t, y, k = me.d, me.c, me.t, me.y, me.k
+    n_img, n_txt = sizes
+    img_all, txt_all = 2 * zn * n_img, 2 * zn * n_txt
+    rows_w, width = wa.shape[2:]
+    wide = gains.shape[-1]
+    col = heads * wide
+    ahead = list(range(1, zn))
+
+    ff = up.shape[2] // zn
+    cuts = {}
+    for s in ahead + [0]:
+        cols = pl.ds(pl.multiple_of(me.ahead(s) * ff, ff), ff)
+        for kind, w in enumerate((up, down)):
+            cuts[s, kind] = local(w.at[:, :, cols], cbuf.at[s, kind], uloc.at[s, kind])
+    row_of = [(c * 2 + half) * n_img for half in range(2)]
+    loads = [
+        local(xi.at[half], xo.at[pl.ds(pl.multiple_of(row_of[half], n_img), n_img)], loc.at[half])
+        for half in range(2)
+    ]
+    loads.append(local(xi.at[t], xr.at[pl.ds(0, n_img)], loc.at[2]))
+    loads.append(local(txt4.at[c, t], xr.at[pl.ds(n_img, n_txt)], loc.at[3]))
+    load_c = local(ci, bx, loc.at[4])
+
     me.greet()
-    y, k = me.y, me.k
-    c = me.c
-    grads, outs = (da, du, dd), (ra, ru, rd)
-    order = [5, 4, 3, 2, 1, 0]
-    rows = own.shape[3]
-    first = {}
-    for chunk in order:
-        kind, st = divmod(chunk, 2)
-        g = grads[kind]
-        group = []
-        for j, yy in enumerate((1 - y, y)):
-            theirs = g.at[st, pl.ds((yy * 2 + 1 - k) * zn, zn)]
-            mine = g.at[st, pl.ds((yy * 2 + k) * zn, zn)]
-            group.append(
-                (
-                    remote(theirs, crecv.at[chunk, j], cs.at[chunk, j], cr.at[chunk, j], {DP: me.d_core}),
-                    local(mine, own.at[chunk, j], loc.at[chunk, j]),
-                )
-            )
-        first[chunk] = group
-    second = {}
-
-    def add(dst, one, two):
-        @pl.loop(0, zn)
-        def _(z):
-            @pl.loop(0, rows // CHUNK)
-            def _(i):
-                at = pl.ds(pl.multiple_of(i * CHUNK, CHUNK), CHUNK)
-                dst[z, at] = (one[z, at].astype(F32) + two[z, at].astype(F32)).astype(BF)
-
-    for chunk in order:
-        for j in range(2):
-            for copy in first[chunk][j]:
-                copy.wait()
-            add(part.at[chunk, j], own.at[chunk, j], crecv.at[chunk, j])
-            if j == 0:
-                second[chunk] = remote(
-                    part.at[chunk, 0], yrecv.at[chunk], ys.at[chunk], yr.at[chunk], {DP: me.d_y}
-                )
-    last = []
-    for chunk in order:
-        kind, st = divmod(chunk, 2)
-        second[chunk].wait()
-        add(own.at[chunk, 0], part.at[chunk, 1], yrecv.at[chunk])
-        for s in range(1, zn):
-            last.append(
+    mine = pl.ds(pl.multiple_of((c * 2 + t) * n_img, n_img), n_img)
+    tokens = [
+        remote(xi.at[t], xo.at[mine], tzs.at[s], tzr.at[s], {CTX: me.ahead(s)}) for s in ahead
+    ]
+    value = cond[...].astype(F32)
+    act = (value / (1.0 + jnp.exp(-value))).astype(BF)
+    for st in range(2):
+        for which in range(6):
+            part = dot(act, modw[st, which].astype(BF), (1, 0))
+            for seq in range(part.shape[0]):
+                mp[seq, st * 6 + which] = part[seq]
+    m_y = remote(mp.at[pl.ds((1 - y) * 2, 2)], my, ms.at[0], mr.at[0], {DP: me.d_y})
+    weights = []
+    block = pl.ds(pl.multiple_of((d * zn + c) * rows_w, rows_w), rows_w)
+    for st in range(2):
+        for kind in range(4):
+            whole = (qkv[st, kind] if kind < 3 else out[st]).astype(BF)
+            for z in range(zn):
+                wa[z, st, :, kind * col : (kind + 1) * col] = whole[:, z * col : (z + 1) * col]
+        weights.append(
+            [
                 remote(
-                    own.at[chunk, 0, me.ahead(s)],
-                    outs[kind].at[c, st],
-                    zs.at[chunk, s],
-                    zr.at[chunk, s],
+                    wa.at[me.ahead(s), st], ga.at[st, block], azs.at[st, s], azr.at[st, s],
                     {CTX: me.ahead(s)},
                 )
+                for s in ahead
+            ]
+        )
+    own_a = [local(wa.at[c, st], ga.at[st, block], loc.at[5 + st]) for st in range(2)]
+    m_y.wait()
+    m2[...] = mp[pl.ds(y * 2, 2)] + my[...]
+    m_c = remote(m2.at[1 - k], mc, ms.at[1], mr.at[1], {DP: me.d_core})
+    m_c.wait()
+    m1[...] = m2[k] + mc[...]
+    m_x = remote(m1, mx, ms.at[2], mr.at[2], {TP: me.t_x})
+    for s in ahead + [0]:
+        for kind in range(2):
+            cuts[s, kind].wait()
+            for st in range(2):
+                pieces[s, kind, st] = cbuf[s, kind, st].astype(BF)
+    m_x.wait()
+    slots[c] = m1[...] + mx[...]
+    m_z = [
+        remote(slots.at[c], slots.at[c], ms.at[2 + s], mr.at[2 + s], {CTX: me.ahead(s)})
+        for s in ahead
+    ]
+    outs = (gu, gd)
+    pairs = [(kind, st) for kind in range(2) for st in range(2)]
+    mlp, own_u = {}, {}
+    for n, (kind, st) in enumerate(pairs):
+        dst = outs[kind].at[st, d * zn + c]
+        mlp[n] = [
+            remote(pieces.at[s, kind, st], dst, uzs.at[n, s], uzr.at[n, s], {CTX: me.ahead(s)})
+            for s in ahead
+        ]
+        own_u[n] = local(pieces.at[0, kind, st], dst, loc.at[7 + n])
+    pending = []
+    over_y = []
+    rows_y = [
+        pl.ds(pl.multiple_of(dd * zn * rows_w, zn * rows_w), zn * rows_w) for dd in (d, me.d_y)
+    ]
+    for st in range(2):
+        for copy in weights[st]:
+            copy.wait()
+        own_a[st].wait()
+        here = ga.at[st, rows_y[0]]
+        over_y.append(remote(here, here, ays.at[st], ayr.at[st], {DP: me.d_y}))
+        pending.append(remote(here, here, acs.at[st, 0], acr.at[st, 0], {DP: me.d_core}))
+    for s in ahead:
+        tokens[s - 1].wait()
+        here = xo.at[pl.ds(pl.multiple_of((me.behind(s) * 2 + t) * n_img, n_img), n_img)]
+        pending.append(remote(here, here, txs.at[s], txr.at[s], {TP: me.t_x}))
+    for st in range(2):
+        over_y[st].wait()
+        there = ga.at[st, rows_y[1]]
+        pending.append(remote(there, there, acs.at[st, 1], acr.at[st, 1], {DP: me.d_core}))
+    for copy in m_z:
+        copy.wait()
+    value = slots[0]
+    for z in range(1, zn):
+        value = value + slots[z]
+    mod[...] = value
+    for copy in loads + pending:
+        copy.wait()
+    saves = [local(ga, ga_o, loc.at[11])]
+
+    at = 0
+    for stream, (rows_in, n) in enumerate(((xo, img_all), (txt, txt_all))):
+
+        @pl.loop(0, n // STEP)
+        def _(i, rows_in=rows_in, stream=stream, at=at):
+            here = pl.ds(pl.multiple_of(i * STEP, STEP), STEP)
+            normed, _ = layer_norm(rows_in[here].astype(F32))
+            value = normed * (1.0 + line(mod, stream, 1)) + line(mod, stream, 0)
+            hidden[pl.ds(pl.multiple_of(at + i * STEP, STEP), STEP)] = value.astype(BF)
+
+        at += n
+    streams = (img_all, txt_all)
+    for stream, first, size in blocks_of(streams, 256):
+        rows = slice(first, first + size)
+        packed[rows] = dot(hidden[rows], ga[stream, :, : 3 * col], (1, 0))
+    saves.append(local(hidden, hidden_o, loc.at[12]))
+    saves.append(local(packed, packed_o, loc.at[13]))
+    fill_heads(packed, gains, streams, heads, q_s, k_s, v_s)
+    flat[...] = jnp.zeros_like(flat)
+    size = (img_all + txt_all) // 4
+    scale = wide ** (-0.5)
+    lanes = flat.shape[1]
+    for head in range(heads):
+
+        @pl.loop(0, 4)
+        def _(i, head=head):
+            rows = pl.ds(pl.multiple_of(i * size, STEP), size)
+            scores = dot(q_s[head, rows], k_s[head], (1, 1)) * scale
+            index = lax.broadcasted_iota(jnp.int32, scores.shape, 1)
+            scores = jnp.where(index < live, scores, EXP_MIN)
+            peak = jnp.max(scores, axis=-1, keepdims=True)
+            log_total = peak + jnp.log(jnp.sum(jnp.exp(scores - peak), axis=-1, keepdims=True))
+            probs = jnp.exp(scores - log_total).astype(BF)
+            lse[rows, head : head + 1] = log_total
+            value = dot(probs, v_s[head], (1, 0))
+            attended[rows, head * wide : (head + 1) * wide] = value
+            lane = lanes - (heads - head) * wide
+            flat[rows, lane : lane + wide] = value.astype(BF)
+
+    saves.append(local(lse, lse_o, loc.at[14]))
+    saves.append(local(attended, att_o, loc.at[15]))
+
+    sent = {}
+    for s in ahead + [0]:
+        zb = me.ahead(s)
+        rows = pl.ds(pl.multiple_of(zb * 2 * n_img, 2 * n_img), 2 * n_img)
+        pim[rows] = dot(flat[rows], ga[0, :, width - lanes :], (1, 1)).astype(BF)
+        rows = pl.ds(pl.multiple_of(img_all + zb * 2 * n_txt, STEP), 2 * n_txt)
+        part = dot(flat[rows], ga[1, :, width - lanes :], (1, 1))
+        for half in range(2):
+            ptx[zb, half] = part[half * n_txt : (half + 1) * n_txt].astype(BF)
+        theirs = pl.ds(pl.multiple_of((zb * 2 + me.t_x) * n_img, n_img), n_img)
+        sent[s] = [
+            remote(pim.at[theirs], recvx.at[s, pl.ds(0, n_img)], sxs.at[s, 0], sxr.at[s, 0], {TP: me.t_x}),
+            remote(ptx.at[zb, me.t_x], recvx.at[s, pl.ds(n_img, n_txt)], sxs.at[s, 1], sxr.at[s, 1], {TP: me.t_x}),
+        ]
+    u_y, u_pending = [], []
+
+    def weights_on(n):
+        kind, st = pairs[n]
+        for copy in mlp[n]:
+            copy.wait()
+        own_u[n].wait()
+        here = outs[kind].at[st, pl.ds(d * zn, zn)]
+        u_y.append(remote(here, here, uys.at[n], uyr.at[n], {DP: me.d_y}))
+        u_pending.append(remote(here, here, ucs.at[n, 0], ucr.at[n, 0], {DP: me.d_core}))
+
+    def weights_last(n):
+        kind, st = pairs[n]
+        u_y[n].wait()
+        there = outs[kind].at[st, pl.ds(me.d_y * zn, zn)]
+        u_pending.append(remote(there, there, ucs.at[n, 1], ucr.at[n, 1], {DP: me.d_core}))
+
+    zc = []
+    for s in ahead + [0]:
+        zb = me.ahead(s)
+        for copy in sent[s]:
+            copy.wait()
+
+        def put(to, value, s=s):
+            if s:
+                sumb[s, to] = value.astype(BF)
+            else:
+                total[to] = value
+
+        @pl.loop(0, n_img // STEP)
+        def _(i, s=s, zb=zb, put=put):
+            to = pl.ds(pl.multiple_of(i * STEP, STEP), STEP)
+            at = pl.ds(pl.multiple_of((zb * 2 + t) * n_img + i * STEP, STEP), STEP)
+            put(to, pim[at].astype(F32) + recvx[s, to].astype(F32))
+
+        to = pl.ds(n_img, n_txt)
+        put(to, ptx[zb, t].astype(F32) + recvx[s, to].astype(F32))
+        if s:
+            zc.append(remote(sumb.at[s], recvz.at[s], szs.at[s], szr.at[s], {CTX: zb}))
+        weights_on(ahead.index(s) if s else zn - 1)
+    for n in range(zn, 4):
+        weights_on(n)
+    for copy in zc:
+        copy.wait()
+
+    def rows(stream, at):
+        p = total[at]
+        for s in ahead:
+            p = p + recvz[s, at].astype(F32)
+        proj[at] = p
+        value = xr[at].astype(F32) + line(mod, stream, 2) * p
+        resid[at] = value
+        normed, _ = layer_norm(value)
+        hb[at] = (normed * (1.0 + line(mod, stream, 4)) + line(mod, stream, 3)).astype(BF)
+
+    row_loops(sizes, rows)
+    shared = share_start(me, hb, (hi, ht), sizes, gzs, gzr, gxs, gxr, gloc)
+    cots = [
+        remote(ci.at[t], co.at[c, t], czs.at[s], czr.at[s], {CTX: me.ahead(s)}) for s in ahead
+    ]
+    load_c.wait()
+    saves.append(local(bx, co.at[c], loc.at[16]))
+    for n in range(4):
+        weights_last(n)
+    share_end(me, shared, (hi, ht), gxs, gxr)
+    for s in ahead:
+        cots[s - 1].wait()
+        here = co.at[me.behind(s), t]
+        u_pending.append(remote(here, here, cxs.at[s], cxr.at[s], {TP: me.t_x}))
+    for copy in u_pending + saves:
+        copy.wait()
+
+
+def forward(zn, live, sizes, heads, cond, modw, qkv, out, txt, gains, up, down, xi, ci):
+    n_img, n_txt = sizes
+    dim = txt.shape[1]
+    rows, wide_out = out.shape[1:]
+    ff = up.shape[2] // zn
+    wide = gains.shape[-1]
+    col = heads * wide
+    width = 4 * col
+    total, block = 2 * zn * (n_img + n_txt), n_img + n_txt
+    lanes = -(-col // 128) * 128
+    seqs = cond.shape[0]
+    txt4 = txt.reshape(zn, 2, n_txt, dim)
+    weight = (shaped((2, 4 * zn, rows, ff), BF), HBM)
+    return call(
+        functools.partial(forward_kernel, zn, live, sizes, heads),
+        0,
+        [VMEM] * 6 + [HBM] * 5,
+        [
+            (shaped((total, dim), BF), HBM),
+            (shaped((total, 3 * col), F32), HBM),
+            (shaped((total, 128), F32), HBM),
+            (shaped((total, col), F32), HBM),
+            (shaped((2, dim, width), BF), HBM),
+            (shaped((zn, 2, n_img, dim), BF), HBM),
+            (shaped((zn, 2, n_txt, dim), BF), HBM),
+            (shaped((zn, 2, n_img, dim), BF), HBM),
+            weight,
+            weight,
+            (shaped((block, dim), F32), VMEM),
+            (shaped((block, dim), F32), VMEM),
+            (shaped((12, dim), F32), VMEM),
+        ],
+        [
+            pltpu.VMEM((zn, 2, rows, width), BF),
+            pltpu.VMEM((seqs, 12, dim), F32),
+            pltpu.VMEM((zn, 2, 2, rows, ff), F32),
+            pltpu.VMEM((zn, 2, 2, rows, ff), BF),
+            pltpu.VMEM((2, dim, width), BF),
+            pltpu.VMEM((2 * zn * n_img, dim), BF),
+            pltpu.VMEM((block, dim), BF),
+            pltpu.VMEM((total, dim), BF),
+            pltpu.VMEM((total, 3 * col), F32),
+            pltpu.VMEM((total, 128), F32),
+            pltpu.VMEM((total, col), F32),
+            pltpu.VMEM((heads, total, wide), BF),
+            pltpu.VMEM((heads, total, wide), BF),
+            pltpu.VMEM((heads, total, wide), BF),
+            pltpu.VMEM((total, lanes), BF),
+            pltpu.VMEM((2 * zn * n_img, dim), BF),
+            pltpu.VMEM((zn, 2, n_txt, dim), BF),
+            pltpu.VMEM((2, 12, dim), F32),
+            pltpu.VMEM((2, 12, dim), F32),
+            pltpu.VMEM((12, dim), F32),
+            pltpu.VMEM((12, dim), F32),
+            pltpu.VMEM((12, dim), F32),
+            pltpu.VMEM((zn, 12, dim), F32),
+            pltpu.VMEM((zn, block, dim), BF),
+            pltpu.VMEM((zn, block, dim), BF),
+            pltpu.VMEM((zn, block, dim), BF),
+            pltpu.VMEM((block, dim), F32),
+            pltpu.VMEM((block, dim), BF),
+            pltpu.VMEM((2, n_img, dim), BF),
+            DMA((zn,)), DMA((zn,)), DMA((zn,)), DMA((zn,)),
+            DMA((2, zn)), DMA((2, zn)), DMA((2,)), DMA((2,)), DMA((2, 2)), DMA((2, 2)),
+            DMA((2 + zn,)), DMA((2 + zn,)),
+            DMA((4, zn)), DMA((4, zn)), DMA((4,)), DMA((4,)), DMA((4, 2)), DMA((4, 2)),
+            DMA((zn, 2)), DMA((zn, 2)), DMA((zn,)), DMA((zn,)),
+            DMA((2, zn)), DMA((2, zn)), DMA((2, zn)), DMA((2, zn)), DMA((2,)),
+            DMA((zn,)), DMA((zn,)), DMA((zn,)), DMA((zn,)),
+            DMA((17,)), DMA((zn, 2)),
+        ],
+        (cond, modw, qkv, out, txt, gains, up, down, xi, txt4, ci),
+    )
+
+
+def back_kernel(
+    live, sizes, heads, bi, bt, ga, hidden, packed, lse, attended, gains, ai, at_, da, gain_row,
+    q_s, k_s, v_s, g_s, flat, stat, dq, dk, dv, pg,
+):
+    wide = gains.shape[-1]
+    scale = wide ** (-0.5)
+    total = sum(sizes)
+    lanes = flat.shape[1]
+    fill_heads(packed, gains, sizes, heads, q_s, k_s, v_s)
+    flat[...] = jnp.zeros_like(flat)
+    stat[...] = jnp.zeros_like(stat)
+    stat[:total] = lse[...]
+    pg[...] = jnp.zeros_like(pg)
+    first_lane = lanes - heads * wide
+
+    def branch(stream, first, size):
+        ref = bi if stream == 0 else bt
+        base = first if stream == 0 else first - sizes[0]
+        return ref[base : base + size]
+
+    flat[:, first_lane:] = attended[...].astype(BF)
+    for stream, first, size in blocks_of(sizes, 256):
+        rows = slice(first, first + size)
+        grad = dot(branch(stream, first, size), ga[stream, :, ga.shape[2] - lanes :], (1, 0)).astype(BF)
+        for head in range(heads):
+            part = grad[:, first_lane + head * wide : first_lane + (head + 1) * wide]
+            g_s[head, rows] = part
+            value = attended[rows, head * wide : (head + 1) * wide]
+            stat[rows, heads + head : heads + head + 1] = jnp.sum(
+                part.astype(F32) * value, axis=-1, keepdims=True
             )
-        last.append(local(own.at[chunk, 0, c], outs[kind].at[c, st], ls.at[chunk]))
+    across = jnp.transpose(stat[...])
+    size = total // 4
+    for head in range(heads):
+        lse_row = across[head : head + 1, :total]
+        delta_row = across[heads + head : heads + head + 1, :total]
+        for i in range(4):
+            rows = slice(i * size, (i + 1) * size)
+            scores = dot(k_s[head, rows], q_s[head], (1, 1)) * scale
+            probs = jnp.exp(scores - lse_row)
+            if (i + 1) * size > live:
+                index = lax.broadcasted_iota(jnp.int32, scores.shape, 0) + i * size
+                probs = jnp.where(index < live, probs, 0.0)
+            prob_grad = dot(v_s[head, rows], g_s[head], (1, 1))
+            score_grad = (probs * (prob_grad - delta_row) * scale).astype(BF)
+            dk[head, rows] = dot(score_grad, q_s[head], (1, 0))
+            dv[head, rows] = dot(probs.astype(BF), g_s[head], (1, 0))
+            part = dot(score_grad, k_s[head, rows], (0, 0))
+            dq[head] = part if i == 0 else dq[head] + part
+    sums = [[jnp.zeros((1, wide), F32) for _ in range(2)] for _ in range(2)]
+    for stream, first, size in blocks_of(sizes, 64):
+        rows = slice(first, first + size)
+        for head in range(heads):
+            q, q_factor, k, k_factor, _ = head_norms(packed, gains, stream, head, rows, heads)
+            for which, (normed, factor, grad) in enumerate(
+                ((q, q_factor, dq[head, rows]), (k, k_factor, dk[head, rows]))
+            ):
+                sums[stream][which] += jnp.sum(grad * normed, axis=0, keepdims=True)
+                raw = rms_back(grad * gains[stream * 2 + which][None, :], normed, factor)
+                lane = (which * heads + head) * wide
+                pg[rows, lane : lane + wide] = raw.astype(BF)
+            lane = (2 * heads + head) * wide
+            pg[rows, lane : lane + wide] = dv[head, rows].astype(BF)
+    gain_row[...] = jnp.zeros_like(gain_row)
+    for stream in range(2):
+        for which in range(2):
+            lane = (stream * 2 + which) * wide
+            gain_row[:, lane : lane + wide] = sums[stream][which]
+    width = 3 * heads * wide
+    for stream, first, size in blocks_of(sizes, 256):
+        out = ai if stream == 0 else at_
+        base = first if stream == 0 else first - sizes[0]
+        out[base : base + size] = dot(
+            pg[first : first + size, :width], ga[stream, :, :width], (1, 1)
+        ).astype(BF)
+    dim = hidden.shape[1]
+    cut_at = ga.shape[2] - lanes
+    cols = dim // 6
+    at = 0
+    for stream, n in enumerate(sizes):
+        rows = slice(at, at + n)
+        for j in range(6):
+            d = slice(j * cols, (j + 1) * cols)
+            one = dot(hidden[rows, d], pg[rows], (0, 0))
+            ref = bi if stream == 0 else bt
+            two = dot(ref[:, d], flat[rows], (0, 0))
+            da[stream, d, :cut_at] = one[:, :cut_at].astype(BF)
+            over = pg.shape[1] - cut_at
+            da[stream, d, cut_at : cut_at + over] = (one[:, cut_at:] + two[:, :over]).astype(BF)
+            da[stream, d, cut_at + over :] = two[:, over:].astype(BF)
+        at += n
+
+
+def back(live, sizes, heads, bi, bt, ga, hidden, packed, lse, attended, gains):
+    total, dim = hidden.shape
+    wide = gains.shape[-1]
+    lanes = -(-heads * wide // 128) * 128
+    stat_rows = -(-total // 128) * 128
+    return own_call(
+        functools.partial(back_kernel, live, sizes, heads),
+        [VMEM] * 8,
+        [
+            (shaped(bi.shape, BF), VMEM),
+            (shaped(bt.shape, BF), VMEM),
+            (shaped(ga.shape, BF), VMEM),
+            (shaped((1, dim), F32), VMEM),
+        ],
+        [pltpu.VMEM((heads, total, wide), BF)] * 4
+        + [pltpu.VMEM((total, lanes), BF), pltpu.VMEM((stat_rows, 128), F32)]
+        + [pltpu.VMEM((heads, total, wide), F32)] * 3
+        + [pltpu.VMEM((total, -(-3 * heads * wide // 128) * 128), BF)],
+        (bi, bt, ga, hidden, packed, lse, attended, gains),
+        8 * 10**9,
+        4 * 10**7,
+    )
+
+
+def adam_parts(weight, moment, second, gradient):
+    new_moment = beta_one * moment + (1.0 - beta_one) * gradient
+    new_second = beta_two * second + (1.0 - beta_two) * gradient * gradient
+    update = (new_moment * (1.0 / corr_one)) / (
+        jnp.sqrt(new_second * (1.0 / corr_two)) + adam_eps
+    ) + decay_rate * weight
+    return weight - learn_rate * update, new_moment, new_second
+
+
+def adam_rows(ins, outs, n, grad_of, rows):
+    @pl.loop(0, rows // 32)
+    def _(i):
+        at = pl.ds(pl.multiple_of(i * 32, 32), 32)
+        grad = grad_of(at)
+        outs[0, n, at] = grad
+        for j, part in enumerate(adam_parts(ins[0, n, at], ins[1, n, at], ins[2, n, at], grad)):
+            outs[1 + j, n, at] = part
+
+
+def mlp_adam_kernel(zn, *refs):
+    me = Place(zn)
+    take = iter(refs)
+    mlp = [next(take) for _ in range(zn)]
+    weights = [[next(take) for _ in range(3)] for _ in range(2)]
+    results = [[next(take) for _ in range(4)] for _ in range(2)]
+    pbuf, ins, outs, psem, isem, osem = take
+    rows, width = pbuf.shape[3:]
+    loads = [local(mlp[s], pbuf.at[s], psem.at[s]) for s in range(zn)]
+    chunks = [(kind, st, src) for kind in range(2) for st in range(2) for src in range(zn)]
+    copies = {}
+    for n, (kind, st, src) in enumerate(chunks):
+        cols = pl.ds(src * width, width)
+        copies[n] = [
+            local(weights[kind][i].at[st, :, cols], ins.at[i, n], isem.at[i, n]) for i in range(3)
+        ]
+    for copy in loads:
+        copy.wait()
+    last = []
+    for n, (kind, st, src) in enumerate(chunks):
+        piece = me.behind(src)
+        cols = pl.ds(src * width, width)
+        for copy in copies[n]:
+            copy.wait()
+        adam_rows(ins, outs, n, lambda at: pbuf[piece, kind, st, at].astype(F32), rows)
+        last.extend(
+            local(outs.at[j, n], results[kind][j].at[st, :, cols], osem.at[j, n]) for j in range(4)
+        )
     for copy in last:
         copy.wait()
 
 
-def give_back(zn, da, du, dd):
-    rows, width = da.shape[2:]
-    shape = shaped((zn, 2, rows, width), BF)
-    return call(
-        functools.partial(return_kernel, zn),
-        4,
-        [HBM] * 3,
-        [(shape, HBM)] * 3,
+def mlp_adam(zn, pieces, up, down):
+    rows, width = pieces[0].shape[2:]
+    n = 4 * zn
+    return own_call(
+        functools.partial(mlp_adam_kernel, zn),
+        [HBM] * (zn + 6),
+        [(shaped(up[0].shape, F32), HBM)] * 8,
         [
-            pltpu.VMEM((6, 2, zn, rows, width), BF),
-            pltpu.VMEM((6, 2, zn, rows, width), BF),
-            pltpu.VMEM((6, 2, zn, rows, width), BF),
-            pltpu.VMEM((6, zn, rows, width), BF),
-            DMA((6, 2)), DMA((6, 2)), DMA((6, 2)), DMA((6,)), DMA((6,)),
-            DMA((6, zn)), DMA((6, zn)), DMA((6,)),
+            pltpu.VMEM((zn, 2, 2, rows, width), BF),
+            pltpu.VMEM((3, n, rows, width), F32),
+            pltpu.VMEM((4, n, rows, width), F32),
+            DMA((zn,)), DMA((3, n)), DMA((4, n)),
         ],
-        (da, du, dd),
-    )
-
-
-def dot(one, two, dims):
-    return lax.dot_general(one, two, ((dims[:1], dims[1:]), ((), ())), preferred_element_type=F32)
+        (*pieces, *up, *down),
+        10**8,
+        36 * 10**6,
+    )
+
+
+def att_adam_kernel(zn, *refs):
+    me = Place(zn)
+    take = iter(refs)
+    pieces = [next(take) for _ in range(zn)]
+    qkv, out = [next(take) for _ in range(3)], [next(take) for _ in range(3)]
+    qkv_new, out_new = [next(take) for _ in range(4)], [next(take) for _ in range(4)]
+    pbuf, grad, ins, outs, psem, isem, osem = take
+    rows, wide = grad.shape[1:]
+    col = wide // zn
+    loads = [local(pieces[s].at[0], pbuf.at[s], psem.at[s]) for s in range(zn)]
+    chunks = [(st, kind) for st in range(2) for kind in range(4)]
+
+    def place(three, three_out, st, kind):
+        return three.at[st, kind] if kind < 3 else three_out.at[st]
+
+    copies = {}
+    for n, (st, kind) in enumerate(chunks):
+        copies[n] = [
+            local(place(qkv[i], out[i], st, kind), ins.at[i, n], isem.at[i, n]) for i in range(3)
+        ]
+    for copy in loads:
+        copy.wait()
+    for n, (st, kind) in enumerate(chunks):
+        for src in range(zn):
+            piece = pbuf[me.behind(src), st, :, kind * col : (kind + 1) * col]
+            grad[n, :, src * col : (src + 1) * col] = piece.astype(F32)
+    last = []
+    for n, (st, kind) in enumerate(chunks):
+        for copy in copies[n]:
+            copy.wait()
+        adam_rows(ins, outs, n, lambda at: grad[n, at], rows)
+        last.extend(
+            local(outs.at[j, n], place(qkv_new[j], out_new[j], st, kind), osem.at[j, n])
+            for j in range(4)
+        )
+    for copy in last:
+        copy.wait()
+
+
+def att_adam(zn, pieces, qkv, out):
+    rows, width = pieces[0].shape[2:]
+    wide = out[0].shape[2]
+    return own_call(
+        functools.partial(att_adam_kernel, zn),
+        [HBM] * (zn + 6),
+        [(shaped(qkv[0].shape, F32), HBM)] * 4 + [(shaped(out[0].shape, F32), HBM)] * 4,
+        [
+            pltpu.VMEM((zn, 2, rows, width), BF),
+            pltpu.VMEM((8, rows, wide), F32),
+            pltpu.VMEM((3, 8, rows, wide), F32),
+            pltpu.VMEM((4, 8, rows, wide), F32),
+            DMA((zn,)), DMA((3, 8)), DMA((4, 8)),
+        ],
+        (*pieces, *qkv, *out),
+        10**8,
+        18 * 10**6,
+    )
+
+
+def mod_adam_kernel(cond, sums, w, m, v, grad_out, w_out, m_out, v_out):
+    value = cond[...].astype(F32)
+    act = (value / (1.0 + jnp.exp(-value))).astype(BF).astype(F32)
+    rows = w.shape[2]
+    which = pl.program_id(0)
+    for first in range(0, rows, 16):
+        at = slice(first, first + 16)
+        grad = act[at, 0:1] * sums[0, which][None, :]
+        for seq in range(1, sums.shape[0]):
+            grad = grad + act[at, seq : seq + 1] * sums[seq, which][None, :]
+        grad_out[0, 0, at] = grad
+        for ref, part in zip((w_out, m_out, v_out), adam_parts(w[0, 0, at], m[0, 0, at], v[0, 0, at], grad)):
+            ref[0, 0, at] = part
+
+
+def mod_adam(cond_cols, sums, three):
+    rows, dim = three[0].shape[2:]
+    spec = pl.BlockSpec((1, 1, rows, dim), lambda i: (i // 6, i % 6, 0, 0))
+    return pl.pallas_call(
+        mod_adam_kernel,
+        out_shape=[shaped(three[0].shape, F32)] * 4,
+        grid=(12,),
+        in_specs=[
+            pl.BlockSpec(cond_cols.shape, lambda i: (0, 0)),
+            pl.BlockSpec(sums.shape, lambda i: (0, 0, 0)),
+        ]
+        + [spec] * 3,
+        out_specs=[spec] * 4,
+        cost_estimate=pl.CostEstimate(flops=10**7, bytes_accessed=25 * 10**6, transcendentals=0),
+    )(cond_cols, sums, *three)
 
 
 def split_body(
@@ -1169,146 +1853,66 @@
     seq = lax.axis_index(DP)
     n_seq = lax.axis_size(DP)
 
-    cond_act = jax.nn.silu(cond.astype(F32)).astype(BF)
-    mod_part = product("sm,tmkc->stkc", cond_act, mod_weight[0].astype(BF))
-    mod_part = mod_part.reshape(n_seq, -1, 128)
-
-    qkv_low = qkv_weight[0].astype(BF).reshape(2, rows, 3, zn, col)
-    qkv_low = jnp.transpose(qkv_low, (3, 0, 1, 2, 4)).reshape(zn, 2, rows, 3 * col)
-    out_low = jnp.transpose(out_weight[0].astype(BF).reshape(2, zn, col, rows), (1, 0, 3, 2))
-    wa = jnp.concatenate([qkv_low, out_low], axis=3)
-    wu = jnp.transpose(up_weight[0].astype(BF).reshape(2, rows, zn, ff), (2, 0, 1, 3))
-    wd = jnp.transpose(down_weight[0].astype(BF).reshape(2, zn, ff, rows), (1, 0, 3, 2))
-
+    def by_rows(four):
+        return jnp.swapaxes(four[0], 1, 2)
+
+    up_three = [value[0] for value in (up_weight, up_moment, up_second)]
+    down_three = [by_rows(value) for value in (down_weight, down_moment, down_second)]
+    out_three = [by_rows(value) for value in (out_weight, out_moment, out_second)]
+    qkv_three = [by_rows(value) for value in (qkv_weight, qkv_moment, qkv_second)]
+    mod_three = [by_rows(value) for value in (mod_weight, mod_moment, mod_second)]
     cot_rows_txt = jnp.pad(cot_txt[0], ((0, txt_pad - txt_len), (0, 0)))
     txt_rows = jnp.pad(txt_in[0], ((0, txt_pad - txt_len), (0, 0)))
-    ga, gu, gd, xo, co, mod = spread(
-        zn, wa, wu, wd, img_in.reshape(2, n_img, dim), cot_img.reshape(2, n_img, dim), mod_part
-    )
-    wide = 3 * col + col
-    ga = ga.reshape(2, -1, wide)
+    gains = norm_gain[0].reshape(4, head_dim)
+    streams = (img_all, txt_pad)
+    live = img_all + txt_len
+    hidden, packed, lse, attended, ga, hi, ht, co, gu, gd, resid, proj_rows, mod = forward(
+        zn, live, sizes, heads, cond, mod_three[0], qkv_three[0], out_three[0], txt_rows, gains,
+        up_three[0], down_three[0], img_in.reshape(2, n_img, dim), cot_img.reshape(2, n_img, dim),
+    )
     gu = gu.reshape(2, -1, ff)
     gd = gd.reshape(2, -1, ff)
-    qkv_full = [ga[st, :, : 3 * col] for st in range(2)]
-    out_full = [ga[st, :, 3 * col :] for st in range(2)]
-    mod = mod.reshape(12, dim)
-    mods = [[mod[st * 6 + which][None, :] for which in range(6)] for st in range(2)]
-
     def own_rows(img, txt):
         one = lax.dynamic_slice_in_dim(img, t * n_img, n_img, 0)
         two = lax.dynamic_slice_in_dim(txt, (c * 2 + t) * n_txt, n_txt, 0)
         return jnp.concatenate([one, two], axis=0)
 
     x_rows = own_rows(img_in[0], txt_rows)
-    cot_rows = own_rows(cot_img[0], cot_rows_txt)
-    tokens = [xo.reshape(img_all, dim), txt_rows]
-    cots = [co.reshape(img_all, dim), cot_rows_txt]
-
-    hidden, packed = [], []
-    for st in range(2):
-        normed, _ = layer_norm(tokens[st].astype(F32))
-        hidden.append((normed * (1.0 + mods[st][1]) + mods[st][0]).astype(BF))
-        packed.append(dot(hidden[st], qkv_full[st], (1, 0)))
-    lengths = (img_all, txt_pad)
-    packs = [p.reshape(n, 3, heads, head_dim) for p, n in zip(packed, lengths)]
-    q_norm = [rms_norm(p[:, 0]) for p in packs]
-    k_norm = [rms_norm(p[:, 1]) for p in packs]
-    gains = norm_gain[0]
-
-    def by_head(pair):
-        return jnp.transpose(jnp.concatenate(pair, axis=0), (1, 0, 2))
-
-    queries = by_head([(q_norm[st][0] * gains[st, 0]).astype(BF) for st in range(2)])
-    keys = by_head([(k_norm[st][0] * gains[st, 1]).astype(BF) for st in range(2)])
-    values = by_head([packs[st][:, 2].astype(BF) for st in range(2)])
-    live = jnp.arange(img_all + txt_pad) < img_all + txt_len
-    scores = product("hqd,hkd->hqk", queries, keys) * scale_factor
-    scores = jnp.where(live[None, None, :], scores, -1e30)
-    peak = jnp.max(scores, axis=-1, keepdims=True)
-    log_total = peak + jnp.log(jnp.sum(jnp.exp(scores - peak), axis=-1, keepdims=True))
-    probs = jnp.exp(scores - log_total)
-    probs_low = probs.astype(BF)
-    attended = product("hqk,hkd->hqd", probs_low, values)
-    flat = jnp.transpose(attended.astype(BF), (1, 0, 2)).reshape(-1, col)
-    flats = [flat[:img_all], flat[img_all:]]
-
     def blocks(img, txt):
         return img.reshape(zn, 2, n_img, dim), txt.reshape(zn, 2, n_txt, dim)
 
-    proj = [dot(flats[st], out_full[st], (1, 1)).astype(BF) for st in range(2)]
-    hi, ht, resid, proj_rows = middle(zn, sizes, *blocks(*proj), x_rows, mod)
-
-    hidden_m = [hi.reshape(img_all, dim), ht.reshape(txt_pad, dim)]
-    mlp_out, mlp_in, du, dd = [], [], [], []
-    for st in range(2):
-        pre_act = dot(hidden_m[st], gu[st], (1, 0))
-        activated, pull = jax.vjp(gelu_tanh, pre_act)
-        activated = activated.astype(BF)
-        mlp_out.append(dot(activated, gd[st], (1, 1)).astype(BF))
-        branch = (cots[st].astype(F32) * mods[st][5]).astype(BF)
-        pre_grad = pull(dot(branch, gd[st], (1, 0)))[0].astype(BF)
-        mlp_in.append(dot(pre_grad, gu[st], (1, 1)).astype(BF))
-        dd.append(dot(branch, activated, (0, 0)).astype(BF))
-        du.append(dot(hidden_m[st], pre_grad, (0, 0)).astype(BF))
-    bi, bt, out_rows, rgrad, sums = turn(
-        zn, sizes, *blocks(*mlp_in), *blocks(*mlp_out), resid, proj_rows, cot_rows, mod
-    )
-
-    branch_a = [bi.reshape(img_all, dim), bt.reshape(txt_pad, dim)]
-    att_grad = jnp.concatenate([dot(branch_a[st], out_full[st], (1, 0)) for st in range(2)], axis=0)
-    att_grad = jnp.transpose(att_grad.astype(BF).reshape(-1, heads, head_dim), (1, 0, 2))
-    delta = jnp.sum(att_grad.astype(F32) * attended, axis=-1, keepdims=True)
-    prob_grad = product("hqd,hkd->hqk", att_grad, values)
-    score_grad = (probs * (prob_grad - delta) * scale_factor).astype(BF)
-    query_grad = jnp.transpose(product("hqk,hkd->hqd", score_grad, keys), (1, 0, 2))
-    key_grad = jnp.transpose(product("hqk,hqd->hkd", score_grad, queries), (1, 0, 2))
-    value_grad = jnp.transpose(product("hqk,hqd->hkd", probs_low, att_grad), (1, 0, 2))
-    gain_lines, input_part, da = [], [], []
-    for st in range(2):
-        part = slice(0, img_all) if st == 0 else slice(img_all, None)
-        q_grad, k_grad = query_grad[part], key_grad[part]
-        gain_lines.append(jnp.sum(q_grad * q_norm[st][0], axis=(0, 1)))
-        gain_lines.append(jnp.sum(k_grad * k_norm[st][0], axis=(0, 1)))
-        q_raw = rms_back(q_grad * gains[st, 0], *q_norm[st])
-        k_raw = rms_back(k_grad * gains[st, 1], *k_norm[st])
-        packed_grad = jnp.stack([q_raw, k_raw, value_grad[part]], axis=1)
-        packed_grad = packed_grad.reshape(-1, 3 * col).astype(BF)
-        input_part.append(dot(packed_grad, qkv_full[st], (1, 1)).astype(BF))
-        d_qkv = dot(hidden[st], packed_grad, (0, 0)).astype(BF)
-        d_out = dot(branch_a[st], flats[st], (0, 0)).astype(BF)
-        da.append(jnp.concatenate([d_qkv, d_out], axis=1))
-    gain_row = jnp.pad(jnp.concatenate(gain_lines), (0, dim - 4 * head_dim))[None, :]
-    oi, ot, gsum = finish(zn, sizes, *blocks(*input_part), x_rows, rgrad, out_rows, sums, gain_row, mod)
+    bi, bt, out_rows, rgrad, sums, *mlp_back = turn(
+        zn, sizes, hi.reshape(img_all, dim), ht.reshape(txt_pad, dim), co.reshape(img_all, dim),
+        cot_rows_txt, resid, proj_rows, mod, gu, gd,
+    )
+    mlp_grads = over_ctx(zn, mlp_back)
+
+    *input_part, da, gain_row = back(
+        live, streams, heads, bi.reshape(img_all, dim), bt.reshape(txt_pad, dim),
+        ga, hidden, packed, lse, attended, gains,
+    )
+    oi, ot, gsum, *att_back = finish(
+        zn, sizes, *blocks(*input_part), x_rows, rgrad, out_rows, sums, gain_row, mod,
+        da[None],
+    )
+    mlp_new = mlp_adam(zn, mlp_grads, up_three, down_three)
+    att_new = att_adam(zn, over_ctx(zn, att_back), qkv_three, out_three)
+    mod_new = mod_adam(cond.T, gsum[:, :12], mod_three)
     img_out, img_grad = oi[0].reshape(1, img_dev, dim), oi[1].reshape(1, img_dev, dim)
     txt_out = ot[0].reshape(1, txt_pad, dim)[:, :txt_len]
     txt_grad = ot[1].reshape(1, txt_pad, dim)[:, :txt_len]
 
-    def stacked(pair):
-        return jnp.stack(pair).reshape(2, n_seq * zn, rows, -1)
-
-    ra, ru, rd = give_back(zn, stacked(da), stacked(du), stacked(dd))
-    qkv_grad = ra[..., : 3 * col].reshape(zn, 2, rows, 3, col)
-    qkv_grad = jnp.transpose(qkv_grad, (1, 2, 3, 0, 4)).reshape(qkv_weight.shape).astype(F32)
-    out_grad = jnp.transpose(ra[..., 3 * col :], (1, 0, 3, 2)).reshape(out_weight.shape).astype(F32)
-    up_grad = jnp.transpose(ru, (1, 2, 0, 3)).reshape(up_weight.shape).astype(F32)
-    down_grad = jnp.transpose(rd, (1, 0, 3, 2)).reshape(down_weight.shape).astype(F32)
-
     gain_grad = jnp.sum(gsum[:, 12, : 4 * head_dim], axis=0).reshape(norm_gain.shape)
-    mod_rows = gsum[:, :12].reshape(n_seq, 2, 1, 6, dim)
-    cond_col = cond_act.astype(F32)[:, None, :, None, None]
-    mod_grad = jnp.sum(cond_col * mod_rows, axis=0)[None]
+
+    def back_rows(value):
+        return jnp.swapaxes(value, 1, 2)[None]
 
     results = [img_out, txt_out, img_grad, txt_grad]
-    for weight, moment, second, grad in (
-        (mod_weight, mod_moment, mod_second, mod_grad),
-        (qkv_weight, qkv_moment, qkv_second, qkv_grad),
-        (out_weight, out_moment, out_second, out_grad),
-        (up_weight, up_moment, up_second, up_grad),
-        (down_weight, down_moment, down_second, down_grad),
-        (norm_gain, gain_moment, gain_second, gain_grad),
-    ):
-        results.append(grad)
-        results.extend(adam_step(weight, moment, second, grad))
+    results += [back_rows(value) for value in mod_new + att_new]
+    results += [value[None] for value in mlp_new[:4]]
+    results += [back_rows(value) for value in mlp_new[4:]]
+    results.append(gain_grad)
+    results.extend(adam_step(norm_gain, gain_moment, gain_second, gain_grad))
     return tuple(results)
 
 
@@ -1319,7 +1923,7 @@
     return (
         dp == 4
         and tp == 2
-        and zn > 1
+        and zn == 4
         and qkv.shape[0] == 1
         and img.shape[0] == dp
         and heads % (tp * zn) == 0

time: 740 us -> 476 us (0.64)
  Pallas kernels: 524 us -> 439 us
  local copies, waits for them, and re-layouts: 77.7 us -> 10.5 us
  other arithmetic: 65.6 us -> 2.11 us
  matrix products: 58.4 us -> 0 us
  starting transfers between devices: 0 us -> 12.8 us
    pallas_call x5 -> x3, Pallas kernels: 524 us -> 373 us  [call(): pl.pallas_call(kernel, out_shape=[shape for shape, _ in outs], in_specs=i...]
    pallas_call x0 -> x4, Pallas kernels: none -> 66.2 us  [the longest x3 51.3 us: own_call(): pl.pallas_call(kernel, out_shape=[shape for shape, _ in outs], in_specs=i...]
    dot_general x31 -> x0, matrix products: 58.4 us -> none  [the longest x24 46.3 us: dot(): lax.dot_general(one, two, ((dims[:1], dims[1:]), ((), ())), preferred_ele...]
    convert_element_type x19 -> x0, local copies, waits for them, and re-layouts: 29.6 us -> none  [the longest x3 7.7 us: split_body(): jnp.transpose(qkv_grad, (1, 2, 3, 0, 4)).reshape(qkv_weight.shape)]
    sub x6 -> x1, other arithmetic: 29.4 us -> 0.61 us  [adam_step(): return (weight - learn_rate * update, new_moment, new_second)]
    dot_general x9 -> x0, local copies, waits for them, and re-layouts: 22.4 us -> none  [the longest x6 17.7 us: dot(): lax.dot_general(one, two, ((dims[:1], dims[1:]), ((), ())), preferred_ele...]
    ppermute x0 -> x6, starting transfers between devices: none -> 12.8 us  [over_ctx(): lax.ppermute(pieces[s], CTX, [(i, (i + s) % zn) for i in range(zn)])]
    convert_element_type x16 -> x0, other arithmetic: 11 us -> none  [the longest x1 2.61 us: split_body(): jnp.transpose(qkv_grad, (1, 2, 3, 0, 4)).reshape(qkv_weight.shape)]
  transfers between devices with their start and end apart: 0 -> 6, of which waited for: 0 -> 1; matrix products, arithmetic and copies ran while one was open for 0% -> 1% of each run, Pallas kernels for 0% -> 26%
where the time goes in v1:
time: 476 us; the launch traced here: 469 us
  Pallas kernels  439 us (92%)
  starting transfers between devices  12.8 us (3%)
  local copies, waits for them, and re-layouts  10.5 us (2%)
    pallas_call x3, Pallas kernels, call(): pl.pallas_call(kernel, out_shape=[shape for shape, _ in outs], in_specs=i...  373 us
    pallas_call x3, Pallas kernels, own_call(): pl.pallas_call(kernel, out_shape=[shape for shape, _ in outs], in_specs=i...  51.3 us
    pallas_call x1, Pallas kernels, mod_adam(): pl.pallas_call(mod_adam_kernel, out_shape=[shaped(three[0].shape, F32)] *...  14.9 us
    ppermute x6, starting transfers between devices, over_ctx(): lax.ppermute(pieces[s], CTX, [(i, (i + s) % zn) for i in range(zn)])  12.8 us
  transfers between devices with their start and end apart: 6, of which 1 were waited for; matrix products, arithmetic and copies ran while one was open for 1% of the time, Pallas kernels for 26%

profile of v1, /device:TPU:0, one launch (start us, length us, event | category | flops | bytes accessed | tf_op | source)
XLA Modules:
  0.0 468.6 jit_solution(6191280876189052441)
XLA Ops:
  0.7 1.9 pad.7.refs_4_
  2.6 1.9 pad.8.refs_3_
  4.4 197.3 %shard_map.438 = (bf16[704,1536]{1,0:T(8,128)(2,1)}, f32[704,576]{1,0:T(8,128)}, f32[704,128]{1,0:T(8,128)}, f32[704,192]{1,0:T(8,128)}, bf16[2,1536,768]{2,1,0:...) custom-call(bf16[4,48]{1,0:T(4,128)(2,1)} %refs_0_.1, ...), custom_call_target="tpu_custom_call" | custom-call | tf_op jit(solution)/shard_map/pallas_call | solution.py:583
  201.8 0.0 copy-start
  201.8 0.0 copy-start.1
  201.8 106.6 %shard_map.439 = (bf16[4,2,64,1536]{3,2,1,0:T(8,128)(2,1)}, bf16[4,2,24,1536]{3,2,1,0:T(8,128)(2,1)}, bf16[88,1536]{1,0:T(8,128)(2,1)}, f32[88,1536]{1,0:T(8,128...) custom-call(bf16[512,1536]{1,0:T(8,128)(2,1)} %bitcast.143, ...), custom_call_target="tpu_custom_call" | custom-call | tf_op jit(solution)/shard_map/pallas_call | solution.py:583
  308.4 3.6 collective-permute-start.3
  311.9 2.6 collective-permute-start.5
  314.6 0.7 pad_maximum_fusion.x_rows
  315.3 29.8 %shard_map.440 = (bf16[512,1536]{1,0:T(8,128)(2,1)}, bf16[192,1536]{1,0:T(8,128)(2,1)}, bf16[2,1536,768]{2,1,0:T(8,128)(2,1)}, f32[1,1536]{1,0:T(1,128)}) custom-call(bf16[512,1536]{1,0:T(8,128)(2,1)} %bitcast.175, bf16[192,1536]{1,0:T(8,128)(2,1)} %bitcast.176, bf16[2,1536,768]{2,1,0:T(8,128)(2,1)} %get-tuple-element.91.ga, ...), custom_call_target="tpu_custom_call" | custom-call | flops 8000000000 | bytes 40000000 | tf_op jit(solution)/shard_map/pallas_call | solution.py:1178
  345.1 68.9 %shard_map.441 = (bf16[2,2,64,1536]{3,2,1,0:T(8,128)(2,1)}, bf16[2,4,2,24,1536]{4,3,2,1,0:T(8,128)(2,1)}, f32[4,16,1536]{2,1,0:T(8,128)}, bf16[1,2,96,768]{3,2,1...) custom-call(bf16[4,2,64,1536]{3,2,1,0:T(8,128)(2,1)} %bitcast.145, ...), custom_call_target="tpu_custom_call" | custom-call | tf_op jit(solution)/shard_map/pallas_call | solution.py:583
  414.1 2.7 collective-permute-start
  416.7 2.1 collective-permute-start.1
  418.9 1.3 fusion.2
  420.2 0.9 fusion.3
  421.1 0.7 copy.51
  421.8 0.8 slice.32
  422.6 0.8 slice.33
  423.4 3.0 collective-permute-done.refs_1_
  426.5 1.9 collective-permute-start.2
  428.4 0.8 slice_reduce_fusion
  429.2 0.1 reshape.148
  429.2 14.9 %shard_map.442 = (f32[2,6,48,1536]{3,2,1,0:T(8,128)}, f32[2,6,48,1536]{3,2,1,0:T(8,128)}, f32[2,6,48,1536]{3,2,1,0:T(8,128)}, f32[2,6,48,1536]{3,2,1,0:T(8,128)}) custom-call(bf16[48,4]{1,0:T(8,128)(2,1)} %bitcast.156, f32[4,12,1536]{2,1,0:T(8,128)} %bitcast.152, f32[2,6,48,1536]{3,2,1,0:T(8,128)} %bitcast.117, f32[2,6,48,1536]{3,2,1,0:T(8,128)} %bitcast.129, ...), custom_call_target="tpu_custom_call" | custom-call | flops 10000000 | bytes 25000000 | tf_op jit(solution)/shard_map/pallas_call | solution.py:1819
  444.2 0.6 multiply_subtract_fusion
  444.8 0.0 copy-start.8
  444.8 0.7 copy-done.7
  445.5 0.1 copy-done.8
  445.6 8.0 %shard_map.443 = (f32[2,3,96,768]{3,2,1,0:T(8,128)}, f32[2,3,96,768]{3,2,1,0:T(8,128)}, f32[2,3,96,768]{3,2,1,0:T(8,128)}, f32[2,3,96,768]{3,2,1,0:T(8,128)}, f3...) custom-call(bf16[1,2,96,768]{3,2,1,0:T(8,128)(2,1)} %get-tuple-element.110.refs_0_, ...), custom_call_target="tpu_custom_call" | custom-call | flops 100000000 | bytes 18000000 | tf_op jit(solution)/shard_map/pallas_call | solution.py:1178
  453.6 0.8 copy-done.3
  454.4 0.2 copy-done.4
  454.6 0.2 copy-done.5
  454.8 13.5 %shard_map.444 = (f32[2,96,3072]{2,1,0:T(8,128)}, f32[2,96,3072]{2,1,0:T(8,128)}, f32[2,96,3072]{2,1,0:T(8,128)}, f32[2,96,3072]{2,1,0:T(8,128)}, f32[2,96,3072]...) custom-call(bf16[2,2,96,768]{3,2,1,0:T(8,128)(2,1)} %get-tuple-element.122.refs_0_, ...), custom_call_target="tpu_custom_call" | custom-call | flops 100000000 | bytes 36000000 | tf_op jit(solution)/shard_map/pallas_call | solution.py:1178
  (28 shorter events, 0.1 us)
Async XLA Ops:
  201.8 112.8 %copy-start = (bf16[1,154,1536]{2,1,0:T(8,128)(2,1)S(1)}, bf16[1,154,1536]{2,1,0:T(8,128)(2,1)}, u32[]{:S(2)}) copy-start(bf16[1,154,1536]{2,1,0:T(8,128)(2,1)} %param.24) | copy-start | bytes 1419268
  201.8 112.8 %copy-start.1 = (bf16[1,128,1536]{2,1,0:T(8,128)(2,1)S(1)}, bf16[1,128,1536]{2,1,0:T(8,128)(2,1)}, u32[]{:S(2)}) copy-start(bf16[1,128,1536]{2,1,0:T(8,128)(2,1)} %param.23) | copy-start | bytes 1179652
  308.4 145.2 %collective-permute-start.3 = (bf16[2,2,96,768]{3,2,1,0:T(8,128)(2,1)}, bf16[2,2,96,768]{3,2,1,0:T(8,128)(2,1)S(1)}, u32[]{:S(2)}, u32[]{:S(2)}) collective-permute-start(bf16[2,2,96,768]{3,2,1,0:T(8,128)(2,1)} %get-tuple-element.123), channel_id=1, source_target_pairs={{0,2},{2,4},{4,6},{6,0},{1,3},{3,5},{5,7},{7,1},{8,10},{10,12},{12... | collective-permute-start | bytes 1769480 | tf_op jit(solution)/shard_map/ppermute | solution.py:1173
  311.9 141.7 %collective-permute-start.4 = (bf16[2,2,96,768]{3,2,1,0:T(8,128)(2,1)}, bf16[2,2,96,768]{3,2,1,0:T(8,128)(2,1)S(1)}, u32[]{:S(2)}, u32[]{:S(2)}) collective-permute-start(bf16[2,2,96,768]{3,2,1,0:T(8,128)(2,1)} %get-tuple-element.124), channel_id=1, source_target_pairs={{0,4},{2,6},{4,0},{6,2},{1,5},{3,7},{5,1},{7,3},{8,12},{10,14},{12... | collective-permute-start | bytes 1769480 | tf_op jit(solution)/shard_map/ppermute | solution.py:1173
  311.9 141.7 %collective-permute-start.5 = (bf16[2,2,96,768]{3,2,1,0:T(8,128)(2,1)}, bf16[2,2,96,768]{3,2,1,0:T(8,128)(2,1)S(1)}, u32[]{:S(2)}, u32[]{:S(2)}) collective-permute-start(bf16[2,2,96,768]{3,2,1,0:T(8,128)(2,1)} %get-tuple-element.125), channel_id=1, source_target_pairs={{0,6},{2,0},{4,2},{6,4},{1,7},{3,1},{5,3},{7,5},{8,14},{10,8},{12,... | collective-permute-start | bytes 1769480 | tf_op jit(solution)/shard_map/ppermute | solution.py:1173
  414.0 6.1 %copy-start.2 = (bf16[2,2,64,1536]{3,2,1,0:T(8,128)(2,1)S(1)}, bf16[2,2,64,1536]{3,2,1,0:T(8,128)(2,1)}, u32[]{:S(2)}) copy-start(bf16[2,2,64,1536]{3,2,1,0:T(8,128)(2,1)} %get-tuple-element.103) | copy-start | bytes 2359300
  414.1 7.1 %copy-start.11 = (bf16[4,48]{1,0:T(4,128)(2,1)S(1)}, bf16[4,48]{1,0:T(4,128)(2,1)}, u32[]{:S(2)}) copy-start(bf16[4,48]{1,0:T(4,128)(2,1)} %refs_0_.1) | copy-start | bytes 1156
  414.1 12.4 %collective-permute-start = (bf16[1,2,96,768]{3,2,1,0:T(8,128)(2,1)}, bf16[1,2,96,768]{3,2,1,0:T(8,128)(2,1)S(1)}, u32[]{:S(2)}, u32[]{:S(2)}) collective-permute-start(bf16[1,2,96,768]{3,2,1,0:T(8,128)(2,1)} %get-tuple-element.111), channel_id=1, source_target_pairs={{0,2},{2,4},{4,6},{6,0},{1,3},{3,5},{5,7},{7,1},{8,10},{10,12},{12... | collective-permute-start | bytes 884744 | tf_op jit(solution)/shard_map/ppermute | solution.py:1173
  416.7 28.0 %collective-permute-start.1 = (bf16[1,2,96,768]{3,2,1,0:T(8,128)(2,1)}, bf16[1,2,96,768]{3,2,1,0:T(8,128)(2,1)S(1)}, u32[]{:S(2)}, u32[]{:S(2)}) collective-permute-start(bf16[1,2,96,768]{3,2,1,0:T(8,128)(2,1)} %get-tuple-element.112), channel_id=1, source_target_pairs={{0,4},{2,6},{4,0},{6,2},{1,5},{3,7},{5,1},{7,3},{8,12},{10,14},{12... | collective-permute-start | bytes 884744 | tf_op jit(solution)/shard_map/ppermute | solution.py:1173
  426.5 17.6 %copy-start.6 = (bf16[1,2,96,768]{3,2,1,0:T(8,128)(2,1)}, bf16[1,2,96,768]{3,2,1,0:T(8,128)(2,1)S(1)}, u32[]{:S(2)}) copy-start(bf16[1,2,96,768]{3,2,1,0:T(8,128)(2,1)S(1)} %collective-permute-done.refs_1_) | copy-start | bytes 884740
  426.5 18.3 %collective-permute-start.2 = (bf16[1,2,96,768]{3,2,1,0:T(8,128)(2,1)}, bf16[1,2,96,768]{3,2,1,0:T(8,128)(2,1)S(1)}, u32[]{:S(2)}, u32[]{:S(2)}) collective-permute-start(bf16[1,2,96,768]{3,2,1,0:T(8,128)(2,1)} %get-tuple-element.113), channel_id=1, source_target_pairs={{0,6},{2,0},{4,2},{6,4},{1,7},{3,1},{5,3},{7,5},{8,14},{10,8},{12,... | collective-permute-start | bytes 884744 | tf_op jit(solution)/shard_map/ppermute | solution.py:1173
  429.2 14.9 %copy-start.9 = (f32[1,2,2,64]{3,2,1,0:T(2,128)}, f32[1,2,2,64]{3,2,1,0:T(2,128)S(1)}, u32[]{:S(2)}) copy-start(f32[1,2,2,64]{3,2,1,0:T(2,128)S(1)} %reshape.148) | copy-start | bytes 3076
  429.2 14.9 %copy-start.10 = (f32[1,2,2,64]{3,2,1,0:T(2,128)S(1)}, f32[1,2,2,64]{3,2,1,0:T(2,128)}, u32[]{:S(2)}) copy-start(f32[1,2,2,64]{3,2,1,0:T(2,128)} %param.31) | copy-start | bytes 3076
  429.2 14.9 %copy-start.12 = (f32[1,2,2,64]{3,2,1,0:T(2,128)S(1)}, f32[1,2,2,64]{3,2,1,0:T(2,128)}, u32[]{:S(2)}) copy-start(f32[1,2,2,64]{3,2,1,0:T(2,128)} %param.39) | copy-start | bytes 3076
  429.2 14.9 %copy-start.13 = (f32[1,2,2,64]{3,2,1,0:T(2,128)S(1)}, f32[1,2,2,64]{3,2,1,0:T(2,128)}, u32[]{:S(2)}) copy-start(f32[1,2,2,64]{3,2,1,0:T(2,128)} %param.45) | copy-start | bytes 3076
  444.8 0.7 copy-start.7
  444.8 0.8 copy-start.8
  453.6 0.8 copy-start.3
  453.6 1.0 copy-start.4
  453.6 1.2 copy-start.5
